TPU v7x, 768 devices: a whole 4x8x12 slice. The times are simulated.
768 devices in a mesh: tile: 16 (over z_hi, y), col: 48 (over x, z_lo, core).
Axes of the slice: x: 4, y: 8, z: 12 (z_hi: 2, z_lo: 6; z = z_hi * 6 + z_lo), core: 2. Of those that a mesh axis runs over, the one named last changes fastest.
Arguments:
- adjoint_in: float32 [25, 512, 6144], P(None, 'tile', 'col'), may hold values from -6 to 6
- centre: float32 [25, 512, 6144], P(None, 'tile', 'col'), may hold values from 0.2 to 0.6
- side_coeff: float32 [4, 25, 512, 6144], P(None, None, 'tile', 'col'), may hold values from 0.05 to 0.25
- vert_coeff: float32 [2, 25, 512, 6144], P(None, None, 'tile', 'col'), may hold values from 0.05 to 0.25
- land_mask: int32 [25, 512, 6144], P(None, 'tile', 'col'), may hold values 0 or 1
- obs_misfit: float32 [16, 48, 48, 128], P('tile', 'col'), may hold values from -6 to 6
- obs_cell: int32 [16, 48, 48, 128], P('tile', 'col'), may hold values from 0 to 102399
- obs_count: int32 [16, 48, 48], P('tile', 'col'), may hold values from 0 to 128, as said below
- fold_partner: int32 [48], replicated, may hold values from 0 to 47, as said below
- fold_flip: int32 [48], replicated, may hold values 0 or 1
Outputs:
- adjoint_out: float32 [25, 512, 6144], P(None, 'tile', 'col')
Inputs may be any that keep to these rules, and one draw needn't show every extreme that they name: `obs_count`: slots at and beyond the count hold values that are ignored; some destination gets 128 from some source in every draw. `fold_partner`: each tile column appears exactly once.
All inputs are finite; a program needn't handle non-finite values. No bound on the sum of `land_mask` on one device may be relied on, other than what follows from the above.
Results may differ from a plain program's by a relative error of at most 0.0003.
Values sent between devices are 32-bit elements; how exact they have to be, the bound alone decides.
A program may use at most 64 MiB of HBM per device.

v0:
```python
import jax
import jax.numpy as jnp
from jax import lax
from jax.sharding import PartitionSpec as P

LEVELS = 25
ROWS = 32
COLS = 128
STEPS = 2


def padded_2(cells, sides, width):
    for axis, dim in sides:
        count = lax.axis_size(axis)
        head = lax.slice_in_dim(cells, 0, width, axis=dim)
        tail = lax.slice_in_dim(cells, cells.shape[dim] - width, cells.shape[dim], axis=dim)
        cells = jnp.concatenate(
            [
                lax.ppermute(tail, axis, [(i, (i + 1) % count) for i in range(count)]),
                cells,
                lax.ppermute(head, axis, [((i + 1) % count, i) for i in range(count)]),
            ],
            axis=dim,
        )
    return cells


def tile_forcing(misfit, cells, counts):
    usable = jnp.arange(misfit.shape[1])[None, :] < counts[:, None]
    values = jnp.where(usable, misfit, jnp.float32(0.0))
    total = jnp.zeros((LEVELS * ROWS * COLS,), jnp.float32)
    return total.at[cells.reshape(-1)].add(values.reshape(-1))


def body(
    adjoint_in,
    centre,
    side_coeff,
    vert_coeff,
    land_mask,
    obs_misfit,
    obs_cell,
    obs_count,
    fold_partner,
    fold_flip,
):
    received = lax.all_to_all(obs_misfit, "col", split_axis=2, concat_axis=1, tiled=True)
    forcing = tile_forcing(received[0, :, 0, :], obs_cell[0, 0], obs_count[0, 0]).reshape(
        adjoint_in.shape
    )
    adjoint = adjoint_in + forcing
    ocean = land_mask.astype(jnp.float32)
    tile_id = lax.axis_index("tile")
    column_id = lax.axis_index("col")
    tile_count = lax.axis_size("tile")
    last_tile = tile_count - 1
    row_count = adjoint.shape[1]
    row_ids = jnp.arange(row_count)
    keep_south = ((row_ids > 0) | (tile_id > 0)).astype(jnp.float32)[:, None]
    keep_north = ((row_ids < row_count - 1) | (tile_id < last_tile)).astype(jnp.float32)[:, None]
    at_top = tile_id == last_tile
    turned_here = fold_flip[column_id] == 1
    for advance in range(STEPS):
        padded = padded_2(side_coeff * adjoint[None], (("tile", 2), ("col", 3)), 1)
        result = centre * adjoint + padded[0, :, 1:-1, :-2] + padded[1, :, 1:-1, 2:]
        result = result + padded[2, :, :-2, 1:-1] * keep_south + padded[3, :, 2:, 1:-1] * keep_north
        upward = vert_coeff[0] * adjoint
        downward = vert_coeff[1] * adjoint
        result = result + jnp.pad(upward, ((0, 1), (0, 0), (0, 0)))[1:]
        result = result + jnp.pad(downward, ((1, 0), (0, 0), (0, 0)))[:-1]
        values = side_coeff[2, :, -1, :] * adjoint[:, -1, :]
        edge_row = jnp.where(turned_here, values[:, ::-1], values)
        matches = (fold_partner == column_id)[:, None, None]
        arrived = jnp.sum(
            jnp.where(
                matches, lax.all_gather(edge_row[None], "col", axis=0, tiled=True), jnp.float32(0.0)
            ),
            axis=0,
        )
        result = result.at[:, -1, :].add(jnp.where(at_top, arrived, jnp.float32(0.0)))
        adjoint = ocean * result
    return adjoint


def solution(mesh):
    in_specs = (
        P(None, "tile", "col"),
        P(None, "tile", "col"),
        P(None, None, "tile", "col"),
        P(None, None, "tile", "col"),
        P(None, "tile", "col"),
        P("tile", "col", None, None),
        P("tile", "col", None, None),
        P("tile", "col", None),
        P(),
        P(),
    )
    out_specs = P(None, "tile", "col")
    return jax.shard_map(body, mesh=mesh, in_specs=in_specs, out_specs=out_specs, check_vma=False)
```

profile of v0, /device:TPU:56, one launch (start us, length us, event | category | flops | bytes accessed | tf_op | source)
XLA Modules:
  0.0 340.7 jit_solution(2659160348696469491)
XLA Ops:
  0.0 15.4 %all-to-all-start = ((f32[1,1,48,128]{3,1,0,2:T(1,128)}), f32[1,1,48,128]{3,1,0,2:T(1,128)S(1)}, u32[]{:S(2)}, u32[]{:S(2)}) async-start(f32[1,1,48,128]{3,1,0,2:T(1,128)} %bitcast.86), calls=%async_computation | async-start | bytes 49152 | tf_op jit(solution)/shard_map/all_to_all | solution.py:47
  16.2 1.2 fusion.43
  18.0 1.2 dynamic_slice.3
  20.0 5.9 %all-to-all-done = f32[1,1,48,128]{3,1,0,2:T(1,128)S(1)} async-done(((f32[1,1,48,128]{3,1,0,2:T(1,128)}), f32[1,1,48,128]{3,1,0,2:T(1,128)S(1)}, u32[]{:S(2)}, u32[]{:S(2)}) %all-to-all-start) | async-done | bytes 24608 | tf_op jit(solution)/shard_map/all_to_all | solution.py:47
  26.6 32.6 %scatter_custom_fusion = f32[102400]{0:T(1024)S(1)} fusion(s32[6144]{0:T(1024)S(1)} %bitcast.87, f32[6144]{0:T(1024)S(1)} %fusion.33, f32[]{:T(128)} %constant.63.clone.1), kind=kCustom, calls=%fused_computation.58 | custom fusion | flops 6144 | bytes 409604 | tf_op jit(solution)/shard_map/scatter-add | solution.py:32
  59.4 1.8 fusion.27
  61.2 1.1 fusion.42
  63.0 9.2 %collective-permute-start = (f32[4,25,1,128]{3,1,2,0:T(8,128)}, f32[4,25,1,128]{3,1,2,0:T(8,128)S(1)}, u32[]{:S(2)}, u32[]{:S(2)}) collective-permute-start(f32[4,25,1,128]{3,1,2,0:T(8,128)} %get-tuple-element.37), channel_id=1, source_target_pairs={{0,48},{48,96},{96,144},{144,192},{192,240},{240,288},{288,336},{3... | collective-permute-start | bytes 153608 | tf_op jit(solution)/shard_map/ppermute | solution.py:19
  72.2 1.9 collective-permute-start.1
  74.3 82.9 %all-gather.2 = f32[48,25,128]{2,1,0:T(8,128)} all-gather(f32[1,25,128]{2,1,0:T(8,128)S(1)} %select_bitcast_fusion.1), channel_id=2, replica_groups=mesh['tile'=16,'col'=48] {'col'}, dimensions={0}, use_global_device_ids=true | all-gather | bytes 627200 | tf_op jit(solution)/shard_map/all_gather | solution.py:76
  157.4 2.9 fusion.39
  160.3 3.8 %copy.42 = f32[4,25,34,1]{2,0,3,1:T(4,128)} copy(f32[4,25,34,1]{3,1,2,0:T(8,128)} %get-tuple-element.33) | data formatting | bytes 27200 | tf_op jit(solution)/shard_map/slice | solution.py:16
  164.2 2.2 collective-permute-start.2
  166.4 3.9 %copy.44 = f32[4,25,34,1]{2,0,3,1:T(4,128)} copy(f32[4,25,34,1]{3,1,2,0:T(8,128)} %get-tuple-element.34) | data formatting | bytes 27200 | tf_op jit(solution)/shard_map/slice | solution.py:15
  170.3 10.4 %collective-permute-start.3 = (f32[4,25,34,1]{2,0,3,1:T(4,128)}, f32[4,25,34,1]{2,0,3,1:T(4,128)}, u32[]{:S(2)}, u32[]{:S(2)}) collective-permute-start(f32[4,25,34,1]{2,0,3,1:T(4,128)} %copy.44), channel_id=1, source_target_pairs={{1,0},{2,1},{3,2},{4,3},{5,4},{6,5},{7,6},{8,7},{9,8},{10,9},{11,1... | collective-permute-start | bytes 40808 | tf_op jit(solution)/shard_map/ppermute | solution.py:21
  180.7 1.3 select_reduce_fusion.1
  182.0 4.0 %copy.43 = f32[4,25,34,1]{3,1,2,0:T(8,128)} copy(f32[4,25,34,1]{2,0,3,1:T(4,128)} %collective-permute-done.2) | data formatting | bytes 27200 | tf_op jit(solution)/shard_map/ppermute | solution.py:19
  186.0 4.0 %copy.45 = f32[4,25,34,1]{3,1,2,0:T(8,128)} copy(f32[4,25,34,1]{2,0,3,1:T(4,128)} %collective-permute-done.3) | data formatting | bytes 27200 | tf_op jit(solution)/shard_map/ppermute | solution.py:21
  190.0 2.5 fusion.11
  192.6 1.3 fusion.26
  195.8 80.7 %all-gather.3 = f32[48,25,128]{2,1,0:T(8,128)} all-gather(f32[1,25,128]{2,1,0:T(8,128)S(1)} %select_bitcast_fusion), channel_id=3, replica_groups=mesh['tile'=16,'col'=48] {'col'}, dimensions={0}, use_global_device_ids=true | all-gather | bytes 627200 | tf_op jit(solution)/shard_map/all_gather | solution.py:76
  276.5 13.3 %collective-permute-start.4 = (f32[4,25,1,128]{3,1,2,0:T(8,128)S(1)}, f32[4,25,1,128]{3,1,2,0:T(8,128)S(1)}, u32[]{:S(2)}, u32[]{:S(2)}) collective-permute-start(f32[4,25,1,128]{3,1,2,0:T(8,128)S(1)} %get-tuple-element.35), channel_id=1, source_target_pairs={{0,48},{48,96},{96,144},{144,192},{192,240},{240,288},{288,336},{3... | collective-permute-start | bytes 153608 | tf_op jit(solution)/shard_map/ppermute | solution.py:19
  289.8 1.9 collective-permute-start.5
  292.7 11.6 %collective-permute-done.5 = f32[4,25,1,128]{3,1,2,0:T(8,128)S(1)} collective-permute-done((f32[4,25,1,128]{3,1,2,0:T(8,128)S(1)}, f32[4,25,1,128]{3,1,2,0:T(8,128)S(1)}, u32[]{:S(2)}, u32[]{:S(2)}) %collective-permute-start.5) | collective-permute-done | bytes 51232 | tf_op jit(solution)/shard_map/ppermute | solution.py:21
  305.0 2.9 fusion.38
  307.9 3.9 %copy.53 = f32[4,25,34,1]{2,0,3,1:T(4,128)} copy(f32[4,25,34,1]{3,1,2,0:T(8,128)} %get-tuple-element.31) | data formatting | bytes 27200 | tf_op jit(solution)/shard_map/slice | solution.py:16
  311.8 1.9 collective-permute-start.6
  313.7 3.9 %copy.55 = f32[4,25,34,1]{2,0,3,1:T(4,128)} copy(f32[4,25,34,1]{3,1,2,0:T(8,128)} %get-tuple-element.32) | data formatting | bytes 27200 | tf_op jit(solution)/shard_map/slice | solution.py:15
  317.6 10.8 %collective-permute-start.7 = (f32[4,25,34,1]{2,0,3,1:T(4,128)}, f32[4,25,34,1]{2,0,3,1:T(4,128)}, u32[]{:S(2)}, u32[]{:S(2)}) collective-permute-start(f32[4,25,34,1]{2,0,3,1:T(4,128)} %copy.55), channel_id=1, source_target_pairs={{1,0},{2,1},{3,2},{4,3},{5,4},{6,5},{7,6},{8,7},{9,8},{10,9},{11,1... | collective-permute-start | bytes 40808 | tf_op jit(solution)/shard_map/ppermute | solution.py:21
  329.1 4.1 %copy.54 = f32[4,25,34,1]{3,1,2,0:T(8,128)} copy(f32[4,25,34,1]{2,0,3,1:T(4,128)} %collective-permute-done.6) | data formatting | bytes 27200 | tf_op jit(solution)/shard_map/ppermute | solution.py:19
  333.2 4.0 %copy.56 = f32[4,25,34,1]{3,1,2,0:T(8,128)} copy(f32[4,25,34,1]{2,0,3,1:T(4,128)} %collective-permute-done.7) | data formatting | bytes 27200 | tf_op jit(solution)/shard_map/ppermute | solution.py:21
  337.2 2.1 fusion.5
  (58 shorter events, 8.8 us)
Async XLA Ops:
  0.0 59.3 %copy-start.8 = (f32[25,32,128]{2,1,0:T(8,128)S(1)}, f32[25,32,128]{2,1,0:T(8,128)}, u32[]{:S(2)}) copy-start(f32[25,32,128]{2,1,0:T(8,128)} %param.14) | copy-start | bytes 1228804
  0.0 25.9 %all-to-all-start = ((f32[1,1,48,128]{3,1,0,2:T(1,128)}), f32[1,1,48,128]{3,1,0,2:T(1,128)S(1)}, u32[]{:S(2)}, u32[]{:S(2)}) async-start(f32[1,1,48,128]{3,1,0,2:T(1,128)} %bitcast.86), calls=%async_computation | async-start | bytes 49152 | tf_op jit(solution)/shard_map/all_to_all | solution.py:47
  20.0 170.1 %copy-start.12 = (f32[32]{0:T(128)}, f32[32]{0:T(128)S(1)}, u32[]{:S(2)}) copy-start(f32[32]{0:T(128)S(1)} %get-tuple-element.46) | copy-start | bytes 388
  20.0 170.1 %copy-start.13 = (f32[32]{0:T(128)}, f32[32]{0:T(128)S(1)}, u32[]{:S(2)}) copy-start(f32[32]{0:T(128)S(1)} %get-tuple-element.47) | copy-start | bytes 388
  59.3 1.9 copy-start
  62.2 11.9 %copy-start.3 = (f32[4,25,32,128]{3,1,2,0:T(8,128)}, f32[4,25,32,128]{3,1,2,0:T(8,128)S(1)}, u32[]{:S(2)}) copy-start(f32[4,25,32,128]{3,1,2,0:T(8,128)S(1)} %get-tuple-element.39) | copy-start | bytes 4915204
  63.0 94.2 %collective-permute-start = (f32[4,25,1,128]{3,1,2,0:T(8,128)}, f32[4,25,1,128]{3,1,2,0:T(8,128)S(1)}, u32[]{:S(2)}, u32[]{:S(2)}) collective-permute-start(f32[4,25,1,128]{3,1,2,0:T(8,128)} %get-tuple-element.37), channel_id=1, source_target_pairs={{0,48},{48,96},{96,144},{144,192},{192,240},{240,288},{288,336},{3... | collective-permute-start | bytes 153608 | tf_op jit(solution)/shard_map/ppermute | solution.py:19
  72.2 85.0 %collective-permute-start.1 = (f32[4,25,1,128]{3,1,2,0:T(8,128)}, f32[4,25,1,128]{3,1,2,0:T(8,128)S(1)}, u32[]{:S(2)}, u32[]{:S(2)}) collective-permute-start(f32[4,25,1,128]{3,1,2,0:T(8,128)} %get-tuple-element.38), channel_id=1, source_target_pairs={{48,0},{96,48},{144,96},{192,144},{240,192},{288,240},{336,288},{3... | collective-permute-start | bytes 153608 | tf_op jit(solution)/shard_map/ppermute | solution.py:21
  164.2 17.8 %collective-permute-start.2 = (f32[4,25,34,1]{2,0,3,1:T(4,128)}, f32[4,25,34,1]{2,0,3,1:T(4,128)}, u32[]{:S(2)}, u32[]{:S(2)}) collective-permute-start(f32[4,25,34,1]{2,0,3,1:T(4,128)} %copy.42), channel_id=1, source_target_pairs={{0,1},{1,2},{2,3},{3,4},{4,5},{5,6},{6,7},{7,8},{8,9},{9,10},{10,1... | collective-permute-start | bytes 40808 | tf_op jit(solution)/shard_map/ppermute | solution.py:19
  170.3 15.7 %collective-permute-start.3 = (f32[4,25,34,1]{2,0,3,1:T(4,128)}, f32[4,25,34,1]{2,0,3,1:T(4,128)}, u32[]{:S(2)}, u32[]{:S(2)}) collective-permute-start(f32[4,25,34,1]{2,0,3,1:T(4,128)} %copy.44), channel_id=1, source_target_pairs={{1,0},{2,1},{3,2},{4,3},{5,4},{6,5},{7,6},{8,7},{9,8},{10,9},{11,1... | collective-permute-start | bytes 40808 | tf_op jit(solution)/shard_map/ppermute | solution.py:21
  190.0 2.6 copy-start.5
  192.6 2.1 copy-start.1
  276.5 16.3 %collective-permute-start.4 = (f32[4,25,1,128]{3,1,2,0:T(8,128)S(1)}, f32[4,25,1,128]{3,1,2,0:T(8,128)S(1)}, u32[]{:S(2)}, u32[]{:S(2)}) collective-permute-start(f32[4,25,1,128]{3,1,2,0:T(8,128)S(1)} %get-tuple-element.35), channel_id=1, source_target_pairs={{0,48},{48,96},{96,144},{144,192},{192,240},{240,288},{288,336},{3... | collective-permute-start | bytes 153608 | tf_op jit(solution)/shard_map/ppermute | solution.py:19
  289.8 14.6 %collective-permute-start.5 = (f32[4,25,1,128]{3,1,2,0:T(8,128)S(1)}, f32[4,25,1,128]{3,1,2,0:T(8,128)S(1)}, u32[]{:S(2)}, u32[]{:S(2)}) collective-permute-start(f32[4,25,1,128]{3,1,2,0:T(8,128)S(1)} %get-tuple-element.36), channel_id=1, source_target_pairs={{48,0},{96,48},{144,96},{192,144},{240,192},{288,240},{336,288},{3... | collective-permute-start | bytes 153608 | tf_op jit(solution)/shard_map/ppermute | solution.py:21
  292.7 11.8 %copy-start.9 = (f32[4,25,1,128]{3,1,2,0:T(8,128)}, f32[4,25,1,128]{3,1,2,0:T(8,128)S(1)}, u32[]{:S(2)}) copy-start(f32[4,25,1,128]{3,1,2,0:T(8,128)S(1)} %collective-permute-done.4) | copy-start | bytes 153604
  304.3 0.6 copy-start.10
  307.9 20.5 %copy-start.2 = (f32[48,25,128]{2,1,0:T(8,128)S(1)}, f32[48,25,128]{2,1,0:T(8,128)}, u32[]{:S(2)}) copy-start(f32[48,25,128]{2,1,0:T(8,128)} %all-gather.3) | copy-start | bytes 1843204
  311.8 17.3 %collective-permute-start.6 = (f32[4,25,34,1]{2,0,3,1:T(4,128)}, f32[4,25,34,1]{2,0,3,1:T(4,128)}, u32[]{:S(2)}, u32[]{:S(2)}) collective-permute-start(f32[4,25,34,1]{2,0,3,1:T(4,128)} %copy.53), channel_id=1, source_target_pairs={{0,1},{1,2},{2,3},{3,4},{4,5},{5,6},{6,7},{7,8},{8,9},{9,10},{10,1... | collective-permute-start | bytes 40808 | tf_op jit(solution)/shard_map/ppermute | solution.py:19
  317.6 15.6 %collective-permute-start.7 = (f32[4,25,34,1]{2,0,3,1:T(4,128)}, f32[4,25,34,1]{2,0,3,1:T(4,128)}, u32[]{:S(2)}, u32[]{:S(2)}) collective-permute-start(f32[4,25,34,1]{2,0,3,1:T(4,128)} %copy.55), channel_id=1, source_target_pairs={{1,0},{2,1},{3,2},{4,3},{5,4},{6,5},{7,6},{8,7},{9,8},{10,9},{11,1... | collective-permute-start | bytes 40808 | tf_op jit(solution)/shard_map/ppermute | solution.py:21
  329.1 8.2 %copy-start.4 = (f32[25,32,128]{2,0,1:T(8,128)S(1)}, f32[25,32,128]{2,0,1:T(8,128)}, u32[]{:S(2)}) copy-start(f32[25,32,128]{2,0,1:T(8,128)} %get-tuple-element.29) | copy-start | bytes 1228804
  329.1 8.2 %copy-start.7 = (f32[25,32,128]{2,1,0:T(8,128)S(1)}, f32[25,32,128]{2,1,0:T(8,128)}, u32[]{:S(2)}) copy-start(f32[25,32,128]{2,1,0:T(8,128)} %param.15) | copy-start | bytes 1228804
  337.2 2.2 copy-start.11
  337.2 2.2 copy-start.6
where the time goes:
time: 342 us; the launch traced here: 341 us
  blocking collectives  164 us (48%)
  starting transfers between devices  67 us (20%)
  other arithmetic  49.2 us (14%)
  local copies, waits for them, and re-layouts  42.2 us (12%)
  waiting for transfers between devices  17.5 us (5%)
    all_gather x2, blocking collectives, body(): lax.all_gather(edge_row[None], 'col', axis=0, tiled=True)  164 us
    scatter-add x1, other arithmetic, tile_forcing(): return total.at[cells.reshape(-1)].add(values.reshape(-1))  32.6 us
    ppermute x4, starting transfers between devices, padded_2(): lax.ppermute(tail, axis, [(i, (i + 1) % count) for i in range(count)])  26.6 us
    ppermute x4, starting transfers between devices, padded_2(): lax.ppermute(head, axis, [((i + 1) % count, i) for i in range(count)])  25 us
    all_to_all x1, starting transfers between devices, body(): lax.all_to_all(obs_misfit, 'col', split_axis=2, concat_axis=1, tiled=True)  15.4 us
    slice x6, local copies, waits for them, and re-layouts, padded_2(): lax.slice_in_dim(cells, cells.shape[dim] - width, cells.shape[dim], axis=...  14.3 us
    ppermute x4, waiting for transfers between devices, padded_2(): lax.ppermute(head, axis, [((i + 1) % count, i) for i in range(count)])  11.6 us
    ppermute x2, local copies, waits for them, and re-layouts, padded_2(): lax.ppermute(tail, axis, [(i, (i + 1) % count) for i in range(count)])  8.16 us
  transfers between devices with their start and end apart: 9, of which 2 were waited for; matrix products, arithmetic and copies ran while one was open for 7% of the time, Pallas kernels for 0%

commit v1 on v0

v1 whole, which is shorter than its diff:
```python
import functools

import jax
import jax.numpy as jnp
from jax import lax
from jax.experimental import pallas as pl
from jax.experimental.pallas import tpu as pltpu
from jax.sharding import PartitionSpec as P

LEVELS = 25
ROWS = 32
COLS = 128
STEPS = 2
CELL_ROWS = LEVELS * ROWS
VREGS = CELL_ROWS // 8
CHUNK = 8
MESH = pl.DeviceIdType.MESH


def grid_of(n_col):
    return (4, 6, 2) if n_col == 48 else (2, n_col // 4, 2)


def kernel(
    n_tile,
    n_col,
    adj_h,
    cen_h,
    side_h,
    vert_h,
    mask_h,
    mis_h,
    cell_h,
    cnt_s,
    fp_s,
    ff_s,
    out_ref,
    adj,
    cen,
    side,
    vert,
    mask,
    cell,
    mis,
    rows_1h,
    vals_1h,
    acc,
    y_ref,
    r_ref,
    edge_out,
    edge_in,
    col_out,
    col_in,
    line_bufs,
    pick_buf,
    group_bufs,
    load_sem,
    a2a_send,
    a2a_recv,
    edge_send,
    edge_recv,
    col_send,
    col_recv,
    line_send,
    line_recv,
    pick_send,
    pick_recv,
):
    nx, nz, nc = grid_of(n_col)
    ng = nx * nc
    me = lax.axis_index("col")
    t = lax.axis_index("tile")
    at_top = t == n_tile - 1
    core = me % nc
    my_z = (me // nc) % nz
    my_x = me // (nc * nz)
    my_g = my_x * nc + core
    east = (me + 1) % n_col
    west = (me + n_col - 1) % n_col

    loads = [
        pltpu.make_async_copy(src, dst, load_sem.at[i])
        for i, (src, dst) in enumerate(
            [
                (cell_h, cell),
                (adj_h, adj),
                (side_h, side),
                (cen_h, cen),
                (vert_h, vert),
                (mask_h, mask),
                (mis_h.at[me], mis.at[me]),
            ]
        )
    ]
    for load in loads:
        load.start()

    barrier = pltpu.get_barrier_semaphore()

    @pl.loop(1, n_col)
    def _(i):
        pl.semaphore_signal(
            barrier, inc=1, device_id={"col": (me + i) % n_col}, device_id_type=MESH
        )

    @pl.when(t > 0)
    def _():
        pl.semaphore_signal(barrier, inc=1, device_id={"tile": t - 1}, device_id_type=MESH)

    @pl.when(t < n_tile - 1)
    def _():
        pl.semaphore_signal(barrier, inc=1, device_id={"tile": t + 1}, device_id_type=MESH)

    pl.semaphore_wait(
        barrier, n_col - 1 + jnp.where(t > 0, 1, 0) + jnp.where(t < n_tile - 1, 1, 0)
    )

    @pl.loop(1, n_col)
    def _(i):
        peer = (me + i) % n_col
        pltpu.make_async_remote_copy(
            src_ref=mis_h.at[peer],
            dst_ref=mis.at[me],
            send_sem=a2a_send,
            recv_sem=a2a_recv,
            device_id={"col": peer},
            device_id_type=MESH,
        ).start()

    def find(s, found):
        target = fp_s[s]
        return tuple(
            jnp.where(target == (g // nc) * nc * nz + my_z * nc + g % nc, s, found[g])
            for g in range(ng)
        ) + (jnp.where(target == me, s, found[ng]),)

    sources = lax.fori_loop(0, n_col, find, (jnp.int32(0),) * (ng + 1))
    my_source = sources[ng]
    flipped = ff_s[my_source]

    loads[0].wait()
    row_ids = lax.broadcasted_iota(jnp.int32, (CELL_ROWS, COLS), 0)

    @pl.loop(0, n_col)
    def _(s):
        hit = row_ids == (cell[s] >> 7)
        rows_1h[:, pl.ds(pl.multiple_of(s * COLS, COLS), COLS)] = jnp.where(
            hit, jnp.float32(1), jnp.float32(0)
        ).astype(jnp.bfloat16)

    acc[...] = jnp.zeros_like(acc)
    loads[6].wait()
    slots = pltpu.make_async_copy(
        mis.at[pl.ds(0, n_col - 1)], mis.at[pl.ds(0, n_col - 1)], a2a_recv
    )
    slots.wait()

    lane_ids = lax.broadcasted_iota(jnp.int32, (COLS, COLS), 0)
    slot_ids = lax.broadcasted_iota(jnp.int32, (1, COLS), 1)

    @pl.loop(0, n_col)
    def _(s):
        value = jnp.where(slot_ids < cnt_s[s], mis[s], jnp.float32(0))
        high = value.astype(jnp.bfloat16).astype(jnp.float32)
        low = value - high
        hit = lane_ids == (cell[s] & 127)
        columns = pl.ds(pl.multiple_of(s * COLS, COLS), COLS)
        vals_1h[0:COLS, columns] = jnp.where(hit, high, jnp.float32(0)).astype(jnp.bfloat16)
        vals_1h[COLS : 2 * COLS, columns] = jnp.where(hit, low, jnp.float32(0)).astype(
            jnp.bfloat16
        )

    width = CHUNK * COLS

    @pl.loop(0, n_col // CHUNK)
    def _(i):
        columns = pl.ds(pl.multiple_of(i * width, width), width)
        acc[...] += lax.dot_general(
            rows_1h[:, columns],
            vals_1h[:, columns],
            (((1,), (1,)), ((), ())),
            preferred_element_type=jnp.float32,
        )

    loads[1].wait()
    forcing = acc[:, :COLS] + acc[:, COLS:]
    y_ref[...] = adj[...] + forcing.reshape(LEVELS, ROWS, COLS)
    for load in loads[2:6]:
        load.wait()

    lanes = lax.broadcasted_iota(jnp.int32, (LEVELS, ROWS, COLS), 2)
    rows = lax.broadcasted_iota(jnp.int32, (LEVELS, ROWS, COLS), 1)
    q_lane = lax.broadcasted_iota(jnp.int32, (VREGS, 8, COLS), 2)
    q_id = lax.broadcasted_iota(jnp.int32, (VREGS, 8, COLS), 0)
    zero = jnp.float32(0)

    for step in range(STEPS):
        line_buf, group_buf = line_bufs[step], group_bufs[step]

        def copy_to(src, dst, send, recv, where):
            return pltpu.make_async_remote_copy(
                src_ref=src,
                dst_ref=dst,
                send_sem=send,
                recv_sem=recv,
                device_id=where,
                device_id_type=MESH,
            )

        y = y_ref[...]
        north = side[2] * y
        south = side[3] * y
        edge_out[step, 0] = north[:, ROWS - 1, :]
        edge_out[step, 1] = south[:, 0, :]
        to_east = side[0] * y
        to_west = side[1] * y
        for way, product, lane in ((0, to_east, COLS - 1), (1, to_west, 0)):
            edge = product.reshape(VREGS, 8, COLS)[:, :, lane : lane + 1]
            col_out[step, way] = jnp.sum(jnp.where(q_lane == q_id, edge, zero), axis=0)

        go_north = copy_to(
            edge_out.at[step, 0],
            edge_in.at[step, 0],
            edge_send.at[step, 0],
            edge_recv.at[step, 0],
            {"tile": t + 1},
        )
        go_south = copy_to(
            edge_out.at[step, 1],
            edge_in.at[step, 1],
            edge_send.at[step, 1],
            edge_recv.at[step, 1],
            {"tile": t - 1},
        )
        go_east = copy_to(
            col_out.at[step, 0],
            col_in.at[step, 0],
            col_send.at[step, 0],
            col_recv.at[step, 0],
            {"col": east},
        )
        go_west = copy_to(
            col_out.at[step, 1],
            col_in.at[step, 1],
            col_send.at[step, 1],
            col_recv.at[step, 1],
            {"col": west},
        )

        @pl.when(t < n_tile - 1)
        def _():
            go_north.start()

        @pl.when(at_top)
        def _():
            line_buf[my_z] = edge_out[step, 0]

            @pl.loop(1, nz)
            def _(i):
                copy_to(
                    edge_out.at[step, 0],
                    line_buf.at[my_z],
                    line_send.at[step],
                    line_recv.at[step],
                    {"col": my_x * nc * nz + ((my_z + i) % nz) * nc + core},
                ).start()

        go_east.start()
        go_west.start()

        @pl.when(t > 0)
        def _():
            go_south.start()

        up = vert[0] * y
        down = vert[1] * y
        level = jnp.zeros((1, ROWS, COLS), jnp.float32)
        r_ref[...] = (
            cen[...] * y
            + jnp.where(lanes == 0, zero, pltpu.roll(to_east, 1, 2))
            + jnp.where(lanes == COLS - 1, zero, pltpu.roll(to_west, COLS - 1, 2))
            + jnp.where(rows == 0, zero, pltpu.roll(north, 1, 1))
            + jnp.where(rows == ROWS - 1, zero, pltpu.roll(south, ROWS - 1, 1))
            + jnp.concatenate([up[1:], level], axis=0)
            + jnp.concatenate([level, down[:-1]], axis=0)
        )

        @pl.when(at_top)
        def _():
            five = pltpu.make_async_copy(
                line_buf.at[pl.ds(0, nz - 1)],
                line_buf.at[pl.ds(0, nz - 1)],
                line_recv.at[step],
            )
            five.wait()
            for g in range(ng):
                picked = line_buf[(sources[g] // nc) % nz]
                pick_buf[step, g] = picked

            @pl.loop(1, ng)
            def _(i):
                g = (my_g + i) % ng
                copy_to(
                    pick_buf.at[step, g],
                    group_buf.at[my_g],
                    pick_send.at[step],
                    pick_recv.at[step],
                    {"col": (g // nc) * nc * nz + my_z * nc + g % nc},
                ).start()

            group_buf[my_g] = pick_buf[step, my_g]
            seven = pltpu.make_async_copy(
                group_buf.at[pl.ds(0, ng - 1)],
                group_buf.at[pl.ds(0, ng - 1)],
                pick_recv.at[step],
            )
            seven.wait()
            arrived = group_buf[(my_source // (nc * nz)) * nc + my_source % nc]
            turn = COLS - 1 - lax.broadcasted_iota(jnp.int32, (LEVELS, COLS), 1)
            turned = jnp.take_along_axis(arrived, turn, axis=1)
            edge_in[step, 1] = jnp.where(flipped == 1, turned, arrived)

        @pl.when(t > 0)
        def _():
            go_north.wait_recv()
            r_ref[:, 0, :] = r_ref[:, 0, :] + edge_in[step, 0]

        @pl.when(t < n_tile - 1)
        def _():
            go_south.wait_recv()

        r_ref[:, ROWS - 1, :] = r_ref[:, ROWS - 1, :] + edge_in[step, 1]

        go_east.wait_recv()
        go_west.wait_recv()
        from_west = jnp.sum(
            jnp.where(q_lane == q_id, col_in[step, 0][None], zero), axis=2, keepdims=True
        ).reshape(LEVELS, ROWS, 1)
        from_east = jnp.sum(
            jnp.where(q_lane == q_id, col_in[step, 1][None], zero), axis=2, keepdims=True
        ).reshape(LEVELS, ROWS, 1)
        sides = jnp.where(lanes == 0, from_west, jnp.where(lanes == COLS - 1, from_east, zero))
        result = (r_ref[...] + sides) * mask[...].astype(jnp.float32)
        if step < STEPS - 1:
            y_ref[...] = result
        else:
            out_ref[...] = result

        @pl.when(t < n_tile - 1)
        def _():
            go_north.wait_send()

        @pl.when(t > 0)
        def _():
            go_south.wait_send()

        go_east.wait_send()
        go_west.wait_send()

        @pl.when(at_top)
        def _():
            pltpu.make_async_copy(
                line_buf.at[pl.ds(0, nz - 1)],
                line_buf.at[pl.ds(0, nz - 1)],
                line_send.at[step],
            ).wait()
            pltpu.make_async_copy(
                group_buf.at[pl.ds(0, ng - 1)],
                group_buf.at[pl.ds(0, ng - 1)],
                pick_send.at[step],
            ).wait()

    pltpu.make_async_copy(
        mis.at[pl.ds(0, n_col - 1)], mis.at[pl.ds(0, n_col - 1)], a2a_send
    ).wait()


def solution(mesh):
    n_tile, n_col = mesh.shape["tile"], mesh.shape["col"]
    nx, nz, nc = grid_of(n_col)
    ng = nx * nc
    cube = (LEVELS, ROWS, COLS)
    f32 = jnp.float32
    any_space = pl.BlockSpec(memory_space=pl.ANY)
    scalars = pl.BlockSpec(memory_space=pltpu.SMEM)
    dma = pltpu.SemaphoreType.DMA

    def body(adj, cen, side, vert, mask, misfit, cell, count, partner, flip):
        return pl.pallas_call(
            functools.partial(kernel, n_tile, n_col),
            out_shape=jax.ShapeDtypeStruct(cube, f32),
            in_specs=[any_space] * 7 + [scalars] * 3,
            out_specs=pl.BlockSpec(memory_space=pltpu.VMEM),
            scratch_shapes=[
                pltpu.VMEM(cube, f32),
                pltpu.VMEM(cube, f32),
                pltpu.VMEM((4,) + cube, f32),
                pltpu.VMEM((2,) + cube, f32),
                pltpu.VMEM(cube, jnp.int32),
                pltpu.VMEM((n_col, 1, COLS), jnp.int32),
                pltpu.VMEM((n_col, 1, COLS), f32),
                pltpu.VMEM((CELL_ROWS, n_col * COLS), jnp.bfloat16),
                pltpu.VMEM((2 * COLS, n_col * COLS), jnp.bfloat16),
                pltpu.VMEM((CELL_ROWS, 2 * COLS), f32),
                pltpu.VMEM(cube, f32),
                pltpu.VMEM(cube, f32),
                pltpu.VMEM((STEPS, 2, LEVELS, COLS), f32),
                pltpu.VMEM((STEPS, 2, LEVELS, COLS), f32),
                pltpu.VMEM((STEPS, 2, 8, COLS), f32),
                pltpu.VMEM((STEPS, 2, 8, COLS), f32),
                [pltpu.VMEM((nz, LEVELS, COLS), f32)] * STEPS,
                pltpu.VMEM((STEPS, ng, LEVELS, COLS), f32),
                [pltpu.VMEM((ng, LEVELS, COLS), f32)] * STEPS,
                dma((7,)),
                dma,
                dma,
                dma((STEPS, 2)),
                dma((STEPS, 2)),
                dma((STEPS, 2)),
                dma((STEPS, 2)),
                dma((STEPS,)),
                dma((STEPS,)),
                dma((STEPS,)),
                dma((STEPS,)),
            ],
            compiler_params=pltpu.CompilerParams(
                collective_id=0, has_side_effects=True, vmem_limit_bytes=60 * 2**20
            ),
        )(
            adj,
            cen,
            side,
            vert,
            mask,
            misfit.reshape(n_col, 1, COLS),
            cell.reshape(n_col, 1, COLS),
            count.reshape(n_col),
            partner,
            flip,
        )

    in_specs = (
        P(None, "tile", "col"),
        P(None, "tile", "col"),
        P(None, None, "tile", "col"),
        P(None, None, "tile", "col"),
        P(None, "tile", "col"),
        P("tile", "col", None, None),
        P("tile", "col", None, None),
        P("tile", "col", None),
        P(),
        P(),
    )
    out_specs = P(None, "tile", "col")
    return jax.shard_map(body, mesh=mesh, in_specs=in_specs, out_specs=out_specs, check_vma=False)
```

time: 342 us -> 47.3 us (0.14)
  blocking collectives: 164 us -> 0 us
  starting transfers between devices: 67 us -> 0 us
  other arithmetic: 49.2 us -> 0 us
  Pallas kernels: 0 us -> 45.4 us
  local copies, waits for them, and re-layouts: 42.2 us -> 1.78 us
  waiting for transfers between devices: 17.5 us -> 0 us
    all_gather x2 -> x0, blocking collectives: 164 us -> none  [body(): lax.all_gather(edge_row[None], 'col', axis=0, tiled=True)]
    ppermute x8 -> x0, starting transfers between devices: 51.6 us -> none  [the longest x4 26.6 us: padded_2(): lax.ppermute(tail, axis, [(i, (i + 1) % count) for i in range(count)])]
    pallas_call x0 -> x1, Pallas kernels: none -> 45.4 us  [body(): pl.pallas_call(functools.partial(kernel, n_tile, n_col), out_shape=jax.Sh...]
    scatter-add x3 -> x0, other arithmetic: 32.6 us -> none  [the longest x1 32.6 us: tile_forcing(): return total.at[cells.reshape(-1)].add(values.reshape(-1))]
    slice x10 -> x0, local copies, waits for them, and re-layouts: 23.2 us -> none  [the longest x6 14.3 us: padded_2(): lax.slice_in_dim(cells, cells.shape[dim] - width, cells.shape[dim], axis=...]
    ppermute x4 -> x0, local copies, waits for them, and re-layouts: 16.2 us -> none  [the longest x2 8.16 us: padded_2(): lax.ppermute(tail, axis, [(i, (i + 1) % count) for i in range(count)])]
    all_to_all x1 -> x0, starting transfers between devices: 15.4 us -> none  [body(): lax.all_to_all(obs_misfit, 'col', split_axis=2, concat_axis=1, tiled=True)]
    ppermute x8 -> x0, waiting for transfers between devices: 11.6 us -> none  [the longest x4 11.6 us: padded_2(): lax.ppermute(head, axis, [((i + 1) % count, i) for i in range(count)])]
  transfers between devices with their start and end apart: 9 -> 0, of which waited for: 2 -> 0; matrix products, arithmetic and copies ran while one was open for 7% -> 0% of each run, Pallas kernels for 0% -> 0%
where the time goes in v1:
time: 47.3 us; the launch traced here: 47.2 us
  Pallas kernels  45.4 us (96%)
  local copies, waits for them, and re-layouts  1.78 us (4%)
    pallas_call x1, Pallas kernels, body(): pl.pallas_call(functools.partial(kernel, n_tile, n_col), out_shape=jax.Sh...  45.4 us
    unnamed x1, local copies, waits for them, and re-layouts  1.78 us

profile of v1, /device:TPU:56, one launch (start us, length us, event | category | flops | bytes accessed | tf_op | source)
XLA Modules:
  0.0 47.2 jit_solution(7279233174911176563)
XLA Ops:
  0.0 45.4 %shard_map.100 = f32[25,32,128]{2,1,0:T(8,128)} custom-call(f32[25,32,128]{2,1,0:T(8,128)} %adj_h.1, f32[25,32,128]{2,1,0:T(8,128)} %cen_h.1, f32[4,25,32,128]{3,2,1,0:T(8,128)} %side_h.1, f32[2,25,32,128]{3,2,1,0:T(8,128)} %vert_h.1, s32[25,32,128]{2,1,0:T(8,128)} %mask_h.1, f32[48,1,128]{2,1,0:T(1,128)} %bitcast.3, s32[48,1,128]{2,1,0:T(1,128)} %bitcast.4, ...), custom_call_target="tpu_custom_call" | custom-call | tf_op jit(solution)/shard_map/pallas_call | solution.py:389
  45.4 1.8 %copy.12 = f32[25,32,128]{2,1,0:T(8,128)} copy(f32[25,32,128]{2,1,0:T(8,128)} %shard_map.100) | data formatting | bytes 819200

commit v2 on v0

v2 whole, which is shorter than its diff:
```python
import functools

import jax
import jax.numpy as jnp
from jax import lax
from jax.experimental import pallas as pl
from jax.experimental.pallas import tpu as pltpu
from jax.sharding import PartitionSpec as P

LEVELS = 25
ROWS = 32
COLS = 128
CELL_ROWS = LEVELS * ROWS
VREGS = CELL_ROWS // 8
MESH = pl.DeviceIdType.MESH


def grid_of(n_col):
    return (4, 6, 2) if n_col == 48 else (2, n_col // 4, 2)


def copy_to(src, dst, send, recv, where):
    return pltpu.make_async_remote_copy(
        src_ref=src,
        dst_ref=dst,
        send_sem=send,
        recv_sem=recv,
        device_id=where,
        device_id_type=MESH,
    )


def wait_for(ref, sem):
    pltpu.make_async_copy(ref, ref, sem).wait()


def kernel(
    n_tile,
    n_col,
    adj_h,
    cen_h,
    side_h,
    vert_h,
    mask_h,
    mis_h,
    cell_h,
    cnt_s,
    fp_s,
    ff_s,
    out_ref,
    adj,
    cen,
    side,
    vert,
    mask,
    cell,
    plane,
    slots,
    rows_1h,
    vals_1h,
    acc,
    y_ref,
    r_ref,
    fixed_row,
    fixed_col,
    fixed_row_in,
    fixed_col_in,
    row_out,
    row_in,
    col_out,
    col_in,
    corner_out,
    corner_in,
    fold_out,
    fold_in,
    line_bufs,
    pick_bufs,
    group_bufs,
    delta,
    delta_out,
    delta_in,
    load_sem,
    plane_send,
    plane_recv,
    slot_send,
    slot_recv,
    fixed_send,
    fixed_recv,
    halo_send,
    halo_recv,
    line_send,
    line_recv,
    pick_send,
    pick_recv,
    delta_send,
    delta_recv,
):
    nx, nz, nc = grid_of(n_col)
    ng = nx * nc
    f32 = jnp.float32
    zero = f32(0)
    me = lax.axis_index("col")
    t = lax.axis_index("tile")
    core = me % nc
    my_z = (me // nc) % nz
    my_x = me // (nc * nz)
    my_g = my_x * nc + core
    sides = ((me + 1) % n_col, (me + n_col - 1) % n_col)
    tiles = (t + 1, t - 1)
    can_go = (t < n_tile - 1, t > 0)
    can_come = (t > 0, t < n_tile - 1)
    at_top = t == n_tile - 1

    def in_plane(g):
        return (g // nc) * nc * nz + my_z * nc + g % nc

    def on_line(z):
        return my_x * nc * nz + z * nc + core

    loads = [
        pltpu.make_async_copy(src, dst, load_sem.at[i])
        for i, (src, dst) in enumerate(
            [
                (mis_h.at[my_x, :, core], plane.at[my_g]),
                (side_h, side),
                (mask_h, mask),
                (cell_h, cell),
                (adj_h, adj),
                (cen_h, cen),
                (vert_h, vert),
            ]
        )
    ]
    for load in loads:
        load.start()

    for way, outermost in ((0, t < 1), (1, t > n_tile - 2)):

        @pl.when(outermost)
        def _():
            fixed_row_in[way][...] = jnp.zeros((LEVELS, COLS), f32)
            row_in[way][...] = jnp.zeros((2, LEVELS, COLS), f32)
            for across in range(2):
                corner_in[2 * way + across][...] = jnp.zeros((8, COLS), f32)

    barrier = pltpu.get_barrier_semaphore()

    def greet(where):
        pl.semaphore_signal(barrier, inc=1, device_id=where, device_id_type=MESH)

    @pl.loop(1, nz)
    def _(i):
        greet({"col": on_line((my_z + i) % nz)})

    @pl.loop(1, ng)
    def _(i):
        greet({"col": in_plane((my_g + i) % ng)})

    for side_id in sides:
        greet({"col": side_id})
    for way in range(2):

        @pl.when(can_go[way])
        def _():
            greet({"tile": tiles[way]})
            for side_id in sides:
                greet({"tile": tiles[way], "col": side_id})

    pl.semaphore_wait(
        barrier,
        nz - 1 + ng - 1 + 2 + 3 * (jnp.where(t > 0, 1, 0) + jnp.where(t < n_tile - 1, 1, 0)),
    )

    @pl.loop(1, ng)
    def _(i):
        g = (my_g + i) % ng
        copy_to(
            mis_h.at[g // nc, :, g % nc],
            plane.at[my_g],
            plane_send,
            plane_recv,
            {"col": in_plane(g)},
        ).start()

    def find(s, found):
        target = fp_s[s]
        return tuple(jnp.where(target == in_plane(g), s, found[g]) for g in range(ng)) + (
            jnp.where(target == me, s, found[ng]),
        )

    sources = lax.fori_loop(0, n_col, find, (jnp.int32(0),) * (ng + 1))
    my_source = sources[ng]
    flipped = ff_s[my_source]

    lanes = lax.broadcasted_iota(jnp.int32, (LEVELS, ROWS, COLS), 2)
    rows = lax.broadcasted_iota(jnp.int32, (LEVELS, ROWS, COLS), 1)
    q_lane = lax.broadcasted_iota(jnp.int32, (VREGS, 8, COLS), 2)
    q_id = lax.broadcasted_iota(jnp.int32, (VREGS, 8, COLS), 0)
    flat_lane = lax.broadcasted_iota(jnp.int32, (LEVELS, COLS), 1)
    flat_level = lax.broadcasted_iota(jnp.int32, (LEVELS, COLS), 0)
    tile_row = lax.broadcasted_iota(jnp.int32, (8, COLS), 0)
    edge_lane = (COLS - 1, 0)
    land_lane = (0, COLS - 1)
    edge_row = (ROWS - 1, 0)
    land_row = (0, ROWS - 1)

    def pack(cube, lane):
        edge = cube.reshape(VREGS, 8, COLS)[:, :, lane : lane + 1]
        return jnp.sum(jnp.where(q_lane == q_id, edge, zero), axis=0)

    def unpack(tile):
        spread = jnp.where(q_lane == q_id, tile[None], zero)
        return jnp.sum(spread, axis=2, keepdims=True).reshape(LEVELS, ROWS, 1)

    loads[1].wait()
    loads[2].wait()
    ocean = mask[...].astype(f32)
    for way in range(2):
        fixed_col[way][...] = pack(side[way] * ocean, edge_lane[way])
        fixed_row[way][...] = side[2 + way, :, edge_row[way], :] * mask[
            :, edge_row[way], :
        ].astype(f32)
    fixed = [
        copy_to(
            fixed_col[way],
            fixed_col_in[way],
            fixed_send.at[way],
            fixed_recv.at[way],
            {"col": sides[way]},
        )
        for way in range(2)
    ] + [
        copy_to(
            fixed_row[way],
            fixed_row_in[way],
            fixed_send.at[2 + way],
            fixed_recv.at[2 + way],
            {"tile": tiles[way]},
        )
        for way in range(2)
    ]
    for way in range(2):
        fixed[way].start()
        pl.when(can_go[way])(fixed[2 + way].start)

    loads[3].wait()
    row_ids = lax.broadcasted_iota(jnp.int32, (CELL_ROWS, COLS), 0)

    def columns_of(z, g):
        return pl.ds(pl.multiple_of((z * ng + g) * COLS, COLS), COLS)

    @pl.loop(0, nz)
    def _(z):
        for g in range(ng):
            hit = row_ids == (cell[g // nc, z, g % nc] >> 7)
            rows_1h[:, columns_of(z, g)] = jnp.where(hit, f32(1), zero).astype(jnp.bfloat16)

    loads[0].wait()
    wait_for(plane.at[pl.ds(0, ng - 1)], plane_recv)

    for mine in range(nz):

        @pl.when(my_z == mine)
        def _():
            @pl.loop(1, nz)
            def _(i):
                z = (mine + i) % nz
                copy_to(
                    plane.at[:, z],
                    slots[mine],
                    slot_send.at[z],
                    slot_recv.at[mine],
                    {"col": on_line(z)},
                ).start()

            slots[mine][...] = plane[:, mine]

    lane_ids = lax.broadcasted_iota(jnp.int32, (COLS, COLS), 0)
    slot_ids = lax.broadcasted_iota(jnp.int32, (1, COLS), 1)

    def add_slots(z, first):
        @pl.when(my_z != z)
        def _():
            wait_for(slots[z], slot_recv.at[z])

        for g in range(ng):
            count = cnt_s[(g // nc) * nc * nz + z * nc + g % nc]
            value = jnp.where(slot_ids < count, slots[z][g], zero)
            high = value.astype(jnp.bfloat16).astype(f32)
            hit = lane_ids == (cell[g // nc, z, g % nc] & 127)
            for half, part in enumerate((high, value - high)):
                vals_1h[half * COLS : (half + 1) * COLS, g * COLS : (g + 1) * COLS] = jnp.where(
                    hit, part, zero
                ).astype(jnp.bfloat16)
        width = ng * COLS
        term = lax.dot_general(
            rows_1h[:, z * width : (z + 1) * width],
            vals_1h[...],
            (((1,), (1,)), ((), ())),
            preferred_element_type=f32,
        )
        if first:
            acc[...] = term
        else:
            acc[...] += term

    @pl.when(my_z < nz // 2)
    def _():
        for z in range(nz):
            add_slots(z, z == 0)

    @pl.when(my_z >= nz // 2)
    def _():
        for z in range(nz - 1, -1, -1):
            add_slots(z, z == nz - 1)

    loads[4].wait()
    y_ref[...] = adj[...] + (acc[:, :COLS] + acc[:, COLS:]).reshape(LEVELS, ROWS, COLS)

    def fold_start(n):
        line_bufs[n][my_z] = fold_out[n][...]

        @pl.loop(1, nz)
        def _(i):
            copy_to(
                fold_out[n],
                line_bufs[n].at[my_z],
                line_send.at[n],
                line_recv.at[n],
                {"col": on_line((my_z + i) % nz)},
            ).start()

    def fold_pick(n):
        wait_for(line_bufs[n].at[pl.ds(0, nz - 1)], line_recv.at[n])
        for g in range(ng):
            pick_bufs[n][g] = line_bufs[n][(sources[g] // nc) % nz]

        @pl.loop(1, ng)
        def _(i):
            g = (my_g + i) % ng
            copy_to(
                pick_bufs[n].at[g],
                group_bufs[n].at[my_g],
                pick_send.at[n],
                pick_recv.at[n],
                {"col": in_plane(g)},
            ).start()

        group_bufs[n][my_g] = pick_bufs[n][my_g]

    def fold_finish(n):
        wait_for(group_bufs[n].at[pl.ds(0, ng - 1)], pick_recv.at[n])
        arrived = group_bufs[n][(my_source // (nc * nz)) * nc + my_source % nc]
        turned = jnp.take_along_axis(arrived, COLS - 1 - flat_lane, axis=1)
        fold_in[n] = jnp.where(flipped == 1, turned, arrived)

    def interior(y):
        to_east = side[0] * y
        to_west = side[1] * y
        north = side[2] * y
        south = side[3] * y
        up = vert[0] * y
        down = vert[1] * y
        level = jnp.zeros((1, ROWS, COLS), f32)
        r = (
            cen[...] * y
            + jnp.where(lanes == 0, zero, pltpu.roll(to_east, 1, 2))
            + jnp.where(lanes == COLS - 1, zero, pltpu.roll(to_west, COLS - 1, 2))
            + jnp.where(rows == 0, zero, pltpu.roll(north, 1, 1))
            + jnp.where(rows == ROWS - 1, zero, pltpu.roll(south, ROWS - 1, 1))
            + jnp.concatenate([up[1:], level], axis=0)
            + jnp.concatenate([level, down[:-1]], axis=0)
        )
        return r

    for load in loads[5:]:
        load.wait()

    @pl.when(at_top)
    def _():
        fold_out[0][...] = side[2, :, ROWS - 1, :] * y_ref[:, ROWS - 1, :]
        fold_start(0)

    r_ref[...] = interior(y_ref[...])
    for way in range(2):
        col_out[way][0] = pack(side[way] * y_ref[...], edge_lane[way])
        col_out[way][1] = fixed_col[way][...] * pack(r_ref[...], edge_lane[way])
        at = edge_row[way]
        row_out[way][0] = side[2 + way, :, at, :] * y_ref[:, at, :]
        row_out[way][1] = fixed_row[way][...] * r_ref[:, at, :]
        for across in range(2):
            lane = edge_lane[across]
            spot = flat_lane == 4 * flat_level + 3 * way
            level_value = y_ref[:, at, :][:, lane : lane + 1]
            for part, weight in enumerate((side[2 + way, :, at, :], side[across, :, at, :])):
                term = weight[:, lane : lane + 1] * level_value
                corner_out[2 * way + across][part : part + 1, :] = jnp.sum(
                    jnp.where(spot, term, zero), axis=0, keepdims=True
                )

    halos = []
    for way in range(2):
        halos.append(
            copy_to(
                col_out[way],
                col_in[way],
                halo_send.at[way],
                halo_recv.at[way],
                {"col": sides[way]},
            )
        )
        halos[-1].start()
    far = []
    for way in range(2):
        far.append(
            [
                copy_to(
                    row_out[way],
                    row_in[way],
                    halo_send.at[2 + way],
                    halo_recv.at[2 + way],
                    {"tile": tiles[way]},
                )
            ]
            + [
                copy_to(
                    corner_out[2 * way + across],
                    corner_in[2 * way + across],
                    halo_send.at[4 + 2 * way + across],
                    halo_recv.at[4 + 2 * way + across],
                    {"tile": tiles[way], "col": sides[across]},
                )
                for across in range(2)
            ]
        )

        @pl.when(can_go[way])
        def _():
            for copy in far[way]:
                copy.start()

    for way in range(2):
        halos[way].wait_recv()
        fixed[way].wait_recv()

        @pl.when(can_come[way])
        def _():
            fixed[2 + way].wait_recv()
            for copy in far[way]:
                copy.wait_recv()

    def with_sides(r, west, east):
        return r + jnp.where(lanes == 0, west, jnp.where(lanes == COLS - 1, east, zero))

    for way in range(2):
        at = land_row[way]
        r_ref[:, at, :] = r_ref[:, at, :] + row_in[way][0]
    y_ref[...] = with_sides(r_ref[...], unpack(col_in[0][0]), unpack(col_in[1][0])) * mask[
        ...
    ].astype(f32)

    ring = []
    for across in range(2):
        lacked = col_out[1 - across][0]
        for way, sub in ((0, 0), (1, 7)):
            lacked = lacked + jnp.where(tile_row == sub, corner_in[2 * way + across][0:1, :], zero)
        ring.append(col_in[across][1] + fixed_col_in[across][...] * lacked)
    r_ref[...] = with_sides(interior(y_ref[...]), unpack(ring[0]), unpack(ring[1]))
    for way in range(2):
        lacked = row_out[1 - way][0]
        for across in range(2):
            spot = flat_lane == 4 * flat_level + 3 * way
            term = jnp.sum(
                jnp.where(spot, corner_in[2 * way + across][1:2, :], zero), axis=1, keepdims=True
            )
            lacked = lacked + jnp.where(flat_lane == land_lane[across], term, zero)
        at = land_row[way]
        r_ref[:, at, :] = r_ref[:, at, :] + (row_in[way][1] + fixed_row_in[way][...] * lacked)
    out_ref[...] = r_ref[...] * mask[...].astype(f32)

    @pl.when(at_top)
    def _():
        top = ROWS - 1
        fold_pick(0)
        fold_finish(0)
        delta[...] = fold_in[0] * mask[:, top, :].astype(f32)
        fold_out[1][...] = side[2, :, top, :] * (y_ref[:, top, :] + delta[...])
        fold_start(1)
        moves = []
        for way in range(2):
            delta_out[way][...] = side[way, :, top, :] * delta[...]
            moves.append(
                copy_to(
                    delta_out[way],
                    delta_in[way],
                    delta_send.at[way],
                    delta_recv.at[way],
                    {"col": sides[way]},
                )
            )
            moves[way].start()
        level = jnp.zeros((1, COLS), f32)
        up = vert[0, :, top, :] * delta[...]
        down = vert[1, :, top, :] * delta[...]
        change = (
            cen[:, top, :] * delta[...]
            + jnp.concatenate([up[1:], level], axis=0)
            + jnp.concatenate([level, down[:-1]], axis=0)
        )
        for way in range(2):
            moves[way].wait_recv()
            shift = 1 if way == 0 else COLS - 1
            change = change + jnp.where(
                flat_lane == land_lane[way],
                pltpu.roll(delta_in[way][...], shift, 1),
                pltpu.roll(delta_out[way][...], shift, 1),
            )
        below = side[3, :, top, :] * delta[...]
        out_ref[:, top - 1, :] = out_ref[:, top - 1, :] + below * mask[:, top - 1, :].astype(f32)
        fold_pick(1)
        fold_finish(1)
        change = change + fold_in[1]
        out_ref[:, top, :] = out_ref[:, top, :] + change * mask[:, top, :].astype(f32)
        for way in range(2):
            moves[way].wait_send()
            wait_for(line_bufs[way].at[pl.ds(0, nz - 1)], line_send.at[way])
            wait_for(group_bufs[way].at[pl.ds(0, ng - 1)], pick_send.at[way])

    wait_for(plane.at[pl.ds(0, ng - 1)], plane_send)

    @pl.loop(1, nz)
    def _(i):
        wait_for(slots[0], slot_send.at[(my_z + i) % nz])

    for way in range(2):
        halos[way].wait_send()
        fixed[way].wait_send()

        @pl.when(can_go[way])
        def _():
            fixed[2 + way].wait_send()
            for copy in far[way]:
                copy.wait_send()


def solution(mesh):
    n_tile, n_col = mesh.shape["tile"], mesh.shape["col"]
    nx, nz, nc = grid_of(n_col)
    ng = nx * nc
    cube = (LEVELS, ROWS, COLS)
    flat = (LEVELS, COLS)
    f32 = jnp.float32
    any_space = pl.BlockSpec(memory_space=pl.ANY)
    scalars = pl.BlockSpec(memory_space=pltpu.SMEM)
    dma = pltpu.SemaphoreType.DMA

    def body(adj, cen, side, vert, mask, misfit, cell, count, partner, flip):
        return pl.pallas_call(
            functools.partial(kernel, n_tile, n_col),
            out_shape=jax.ShapeDtypeStruct(cube, f32),
            in_specs=[any_space] * 7 + [scalars] * 3,
            out_specs=pl.BlockSpec(memory_space=pltpu.VMEM),
            scratch_shapes=[
                pltpu.VMEM(cube, f32),
                pltpu.VMEM(cube, f32),
                pltpu.VMEM((4,) + cube, f32),
                pltpu.VMEM((2,) + cube, f32),
                pltpu.VMEM(cube, jnp.int32),
                pltpu.VMEM((nx, nz, nc, 1, COLS), jnp.int32),
                pltpu.VMEM((ng, nz, 1, COLS), f32),
                [pltpu.VMEM((ng, 1, COLS), f32)] * nz,
                pltpu.VMEM((CELL_ROWS, n_col * COLS), jnp.bfloat16),
                pltpu.VMEM((2 * COLS, ng * COLS), jnp.bfloat16),
                pltpu.VMEM((CELL_ROWS, 2 * COLS), f32),
                pltpu.VMEM(cube, f32),
                pltpu.VMEM(cube, f32),
                [pltpu.VMEM(flat, f32)] * 2,
                [pltpu.VMEM((8, COLS), f32)] * 2,
                [pltpu.VMEM(flat, f32)] * 2,
                [pltpu.VMEM((8, COLS), f32)] * 2,
                [pltpu.VMEM((2,) + flat, f32)] * 2,
                [pltpu.VMEM((2,) + flat, f32)] * 2,
                [pltpu.VMEM((2, 8, COLS), f32)] * 2,
                [pltpu.VMEM((2, 8, COLS), f32)] * 2,
                [pltpu.VMEM((8, COLS), f32)] * 4,
                [pltpu.VMEM((8, COLS), f32)] * 4,
                [pltpu.VMEM(flat, f32)] * 2,
                pltpu.VMEM((2,) + flat, f32),
                [pltpu.VMEM((nz,) + flat, f32)] * 2,
                [pltpu.VMEM((ng,) + flat, f32)] * 2,
                [pltpu.VMEM((ng,) + flat, f32)] * 2,
                pltpu.VMEM(flat, f32),
                [pltpu.VMEM(flat, f32)] * 2,
                [pltpu.VMEM(flat, f32)] * 2,
                dma((7,)),
                dma,
                dma,
                dma((nz,)),
                dma((nz,)),
                dma((4,)),
                dma((4,)),
                dma((8,)),
                dma((8,)),
                dma((2,)),
                dma((2,)),
                dma((2,)),
                dma((2,)),
                dma((2,)),
                dma((2,)),
            ],
            compiler_params=pltpu.CompilerParams(
                collective_id=0, has_side_effects=True, vmem_limit_bytes=60 * 2**20
            ),
        )(
            adj,
            cen,
            side,
            vert,
            mask,
            misfit.reshape(nx, nz, nc, 1, COLS),
            cell.reshape(nx, nz, nc, 1, COLS),
            count.reshape(n_col),
            partner,
            flip,
        )

    in_specs = (
        P(None, "tile", "col"),
        P(None, "tile", "col"),
        P(None, None, "tile", "col"),
        P(None, None, "tile", "col"),
        P(None, "tile", "col"),
        P("tile", "col", None, None),
        P("tile", "col", None, None),
        P("tile", "col", None),
        P(),
        P(),
    )
    out_specs = P(None, "tile", "col")
    return jax.shard_map(body, mesh=mesh, in_specs=in_specs, out_specs=out_specs, check_vma=False)
```

time: 342 us -> 45.4 us (0.13)
  the two profiles are of different devices: /device:TPU:56 before, /device:TPU:441 now
where the time goes in v2:
time: 45.4 us; the launch traced here: 45.3 us
  Pallas kernels  43.5 us (96%)
  local copies, waits for them, and re-layouts  1.78 us (4%)
    pallas_call x1, Pallas kernels, body(): pl.pallas_call(functools.partial(kernel, n_tile, n_col), out_shape=jax.Sh...  43.5 us
    unnamed x1, local copies, waits for them, and re-layouts  1.78 us

profile of v2, /device:TPU:441, one launch (start us, length us, event | category | flops | bytes accessed | tf_op | source)
XLA Modules:
  0.0 45.3 jit_solution(11350467241631155172)
XLA Ops:
  0.0 43.5 %shard_map.100 = f32[25,32,128]{2,1,0:T(8,128)} custom-call(f32[25,32,128]{2,1,0:T(8,128)} %adj_h.1, f32[25,32,128]{2,1,0:T(8,128)} %cen_h.1, f32[4,25,32,128]{3,2,1,0:T(8,128)} %side_h.1, f32[2,25,32,128]{3,2,1,0:T(8,128)} %vert_h.1, s32[25,32,128]{2,1,0:T(8,128)} %mask_h.1, f32[4,6,2,1,128]{4,3,2,1,0:T(1,128)} %bitcast.3, s32[4,6,2,1,128]{4,3,2,1,0:T(1,128)} %bitcast.4, ...), custom_call_target="tpu_custom_call" | custom-call | tf_op jit(solution)/shard_map/pallas_call | solution.py:558
  43.5 1.8 %copy.12 = f32[25,32,128]{2,1,0:T(8,128)} copy(f32[25,32,128]{2,1,0:T(8,128)} %shard_map.100) | data formatting | bytes 819200

commit v3 on v2

--- a/solution.py
+++ b/solution.py
@@ -12,6 +12,7 @@
 COLS = 128
 CELL_ROWS = LEVELS * ROWS
 VREGS = CELL_ROWS // 8
+PARTS = ((0, 16), (16, LEVELS))
 MESH = pl.DeviceIdType.MESH
 
 
@@ -32,6 +33,12 @@
 
 def wait_for(ref, sem):
     pltpu.make_async_copy(ref, ref, sem).wait()
+
+
+def hand_out(result, out_h, sem):
+    copy = pltpu.make_async_copy(result, out_h, sem)
+    copy.start()
+    copy.wait()
 
 
 def kernel(
@@ -72,10 +79,10 @@
     corner_out,
     corner_in,
     fold_out,
-    fold_in,
     line_bufs,
     pick_bufs,
     group_bufs,
+    top_1h,
     delta,
     delta_out,
     delta_in,
@@ -171,6 +178,8 @@
         nz - 1 + ng - 1 + 2 + 3 * (jnp.where(t > 0, 1, 0) + jnp.where(t < n_tile - 1, 1, 0)),
     )
 
+    far_way = 1 - 2 * (my_z // (nz // 2))
+
     @pl.loop(1, ng)
     def _(i):
         g = (my_g + i) % ng
@@ -278,7 +287,53 @@
     lane_ids = lax.broadcasted_iota(jnp.int32, (COLS, COLS), 0)
     slot_ids = lax.broadcasted_iota(jnp.int32, (1, COLS), 1)
 
-    def add_slots(z, first):
+    def fold_start(n, h):
+        part = 2 * n + h
+        line_bufs[part][my_z] = fold_out[part][...]
+
+        @pl.loop(1, nz)
+        def _(i):
+            z = (my_z + nz + far_way * (nz - i)) % nz
+            copy_to(
+                fold_out[part],
+                line_bufs[part].at[my_z],
+                line_send.at[part],
+                line_recv.at[part],
+                {"col": on_line(z)},
+            ).start()
+
+    def fold_pick(n, h):
+        part = 2 * n + h
+        wait_for(line_bufs[part].at[pl.ds(0, nz - 1)], line_recv.at[part])
+        for g in range(ng):
+            pick_bufs[part][g] = line_bufs[part][(sources[g] // nc) % nz]
+
+        @pl.loop(1, ng)
+        def _(i):
+            g = (my_g + i) % ng
+            copy_to(
+                pick_bufs[part].at[g],
+                group_bufs[part].at[my_g],
+                pick_send.at[part],
+                pick_recv.at[part],
+                {"col": in_plane(g)},
+            ).start()
+
+        group_bufs[part][my_g] = pick_bufs[part][my_g]
+
+    def fold_finish(n, h):
+        part = 2 * n + h
+        count = PARTS[h][1] - PARTS[h][0]
+        wait_for(group_bufs[part].at[pl.ds(0, ng - 1)], pick_recv.at[part])
+        arrived = group_bufs[part][(my_source // (nc * nz)) * nc + my_source % nc]
+        backwards = COLS - 1 - lax.broadcasted_iota(jnp.int32, (count, COLS), 1)
+        turned = jnp.take_along_axis(arrived, backwards, axis=1)
+        return jnp.where(flipped == 1, turned, arrived)
+
+    for load in loads[4:]:
+        load.wait()
+
+    def add_slots(z, first, last):
         @pl.when(my_z != z)
         def _():
             wait_for(slots[z], slot_recv.at[z])
@@ -292,6 +347,29 @@
                 vals_1h[half * COLS : (half + 1) * COLS, g * COLS : (g + 1) * COLS] = jnp.where(
                     hit, part, zero
                 ).astype(jnp.bfloat16)
+
+        def lead():
+            level_ids = lax.broadcasted_iota(jnp.int32, (ROWS, COLS), 0)
+            for g in range(ng):
+                cell_row = cell[g // nc, z, g % nc] >> 7
+                level = jnp.where((cell_row & (ROWS - 1)) == ROWS - 1, cell_row >> 5, -1)
+                top_1h[:, g * COLS : (g + 1) * COLS] = jnp.where(
+                    level_ids == level, f32(1), zero
+                ).astype(jnp.bfloat16)
+            row = lax.dot_general(
+                top_1h[...],
+                vals_1h[...],
+                (((1,), (1,)), ((), ())),
+                preferred_element_type=f32,
+            )[:LEVELS]
+            row = row + acc[...].reshape(LEVELS, ROWS, 2 * COLS)[:, ROWS - 1, :]
+            row = adj[:, ROWS - 1, :] + row[:, :COLS] + row[:, COLS:]
+            for h, (low, high) in enumerate(PARTS):
+                fold_out[h][...] = side[2, low:high, ROWS - 1, :] * row[low:high]
+                fold_start(0, h)
+
+        if last:
+            pl.when(at_top)(lead)
         width = ng * COLS
         term = lax.dot_general(
             rows_1h[:, z * width : (z + 1) * width],
@@ -307,52 +385,14 @@
     @pl.when(my_z < nz // 2)
     def _():
         for z in range(nz):
-            add_slots(z, z == 0)
+            add_slots(z, z == 0, z == nz - 1)
 
     @pl.when(my_z >= nz // 2)
     def _():
         for z in range(nz - 1, -1, -1):
-            add_slots(z, z == nz - 1)
-
-    loads[4].wait()
+            add_slots(z, z == nz - 1, z == 0)
+
     y_ref[...] = adj[...] + (acc[:, :COLS] + acc[:, COLS:]).reshape(LEVELS, ROWS, COLS)
-
-    def fold_start(n):
-        line_bufs[n][my_z] = fold_out[n][...]
-
-        @pl.loop(1, nz)
-        def _(i):
-            copy_to(
-                fold_out[n],
-                line_bufs[n].at[my_z],
-                line_send.at[n],
-                line_recv.at[n],
-                {"col": on_line((my_z + i) % nz)},
-            ).start()
-
-    def fold_pick(n):
-        wait_for(line_bufs[n].at[pl.ds(0, nz - 1)], line_recv.at[n])
-        for g in range(ng):
-            pick_bufs[n][g] = line_bufs[n][(sources[g] // nc) % nz]
-
-        @pl.loop(1, ng)
-        def _(i):
-            g = (my_g + i) % ng
-            copy_to(
-                pick_bufs[n].at[g],
-                group_bufs[n].at[my_g],
-                pick_send.at[n],
-                pick_recv.at[n],
-                {"col": in_plane(g)},
-            ).start()
-
-        group_bufs[n][my_g] = pick_bufs[n][my_g]
-
-    def fold_finish(n):
-        wait_for(group_bufs[n].at[pl.ds(0, ng - 1)], pick_recv.at[n])
-        arrived = group_bufs[n][(my_source // (nc * nz)) * nc + my_source % nc]
-        turned = jnp.take_along_axis(arrived, COLS - 1 - flat_lane, axis=1)
-        fold_in[n] = jnp.where(flipped == 1, turned, arrived)
 
     def interior(y):
         to_east = side[0] * y
@@ -372,14 +412,6 @@
             + jnp.concatenate([level, down[:-1]], axis=0)
         )
         return r
-
-    for load in loads[5:]:
-        load.wait()
-
-    @pl.when(at_top)
-    def _():
-        fold_out[0][...] = side[2, :, ROWS - 1, :] * y_ref[:, ROWS - 1, :]
-        fold_start(0)
 
     r_ref[...] = interior(y_ref[...])
     for way in range(2):
@@ -439,6 +471,11 @@
             for copy in far[way]:
                 copy.start()
 
+    @pl.when(at_top)
+    def _():
+        for h in range(2):
+            fold_pick(0, h)
+
     for way in range(2):
         halos[way].wait_recv()
         fixed[way].wait_recv()
@@ -458,6 +495,29 @@
     y_ref[...] = with_sides(r_ref[...], unpack(col_in[0][0]), unpack(col_in[1][0])) * mask[
         ...
     ].astype(f32)
+
+    top = ROWS - 1
+    moves = [
+        copy_to(
+            delta_out[way],
+            delta_in[way],
+            delta_send.at[way],
+            delta_recv.at[way],
+            {"col": sides[way]},
+        )
+        for way in range(2)
+    ]
+
+    @pl.when(at_top)
+    def _():
+        for h, (low, high) in enumerate(PARTS):
+            edge = mask[low:high, top, :].astype(f32) * fold_finish(0, h)
+            delta[low:high, :] = edge
+            fold_out[2 + h][...] = side[2, low:high, top, :] * (y_ref[low:high, top, :] + edge)
+            fold_start(1, h)
+        for way in range(2):
+            delta_out[way][...] = side[way, :, top, :] * delta[...]
+            moves[way].start()
 
     ring = []
     for across in range(2):
@@ -480,25 +540,6 @@
 
     @pl.when(at_top)
     def _():
-        top = ROWS - 1
-        fold_pick(0)
-        fold_finish(0)
-        delta[...] = fold_in[0] * mask[:, top, :].astype(f32)
-        fold_out[1][...] = side[2, :, top, :] * (y_ref[:, top, :] + delta[...])
-        fold_start(1)
-        moves = []
-        for way in range(2):
-            delta_out[way][...] = side[way, :, top, :] * delta[...]
-            moves.append(
-                copy_to(
-                    delta_out[way],
-                    delta_in[way],
-                    delta_send.at[way],
-                    delta_recv.at[way],
-                    {"col": sides[way]},
-                )
-            )
-            moves[way].start()
         level = jnp.zeros((1, COLS), f32)
         up = vert[0, :, top, :] * delta[...]
         down = vert[1, :, top, :] * delta[...]
@@ -517,14 +558,19 @@
             )
         below = side[3, :, top, :] * delta[...]
         out_ref[:, top - 1, :] = out_ref[:, top - 1, :] + below * mask[:, top - 1, :].astype(f32)
-        fold_pick(1)
-        fold_finish(1)
-        change = change + fold_in[1]
-        out_ref[:, top, :] = out_ref[:, top, :] + change * mask[:, top, :].astype(f32)
+        delta[...] = change
+        for h in range(2):
+            fold_pick(1, h)
+        for h, (low, high) in enumerate(PARTS):
+            total = delta[low:high, :] + fold_finish(1, h)
+            out_ref[low:high, top, :] = out_ref[low:high, top, :] + total * mask[
+                low:high, top, :
+            ].astype(f32)
         for way in range(2):
             moves[way].wait_send()
-            wait_for(line_bufs[way].at[pl.ds(0, nz - 1)], line_send.at[way])
-            wait_for(group_bufs[way].at[pl.ds(0, ng - 1)], pick_send.at[way])
+        for part in range(4):
+            wait_for(line_bufs[part].at[pl.ds(0, nz - 1)], line_send.at[part])
+            wait_for(group_bufs[part].at[pl.ds(0, ng - 1)], pick_send.at[part])
 
     wait_for(plane.at[pl.ds(0, ng - 1)], plane_send)
 
@@ -549,15 +595,16 @@
     ng = nx * nc
     cube = (LEVELS, ROWS, COLS)
     flat = (LEVELS, COLS)
+    parts = [(high - low, COLS) for low, high in PARTS] * 2
     f32 = jnp.float32
     any_space = pl.BlockSpec(memory_space=pl.ANY)
     scalars = pl.BlockSpec(memory_space=pltpu.SMEM)
     dma = pltpu.SemaphoreType.DMA
 
     def body(adj, cen, side, vert, mask, misfit, cell, count, partner, flip):
-        return pl.pallas_call(
+        result = pl.pallas_call(
             functools.partial(kernel, n_tile, n_col),
-            out_shape=jax.ShapeDtypeStruct(cube, f32),
+            out_shape=pltpu.VMEM(cube, f32),
             in_specs=[any_space] * 7 + [scalars] * 3,
             out_specs=pl.BlockSpec(memory_space=pltpu.VMEM),
             scratch_shapes=[
@@ -584,11 +631,11 @@
                 [pltpu.VMEM((2, 8, COLS), f32)] * 2,
                 [pltpu.VMEM((8, COLS), f32)] * 4,
                 [pltpu.VMEM((8, COLS), f32)] * 4,
-                [pltpu.VMEM(flat, f32)] * 2,
-                pltpu.VMEM((2,) + flat, f32),
-                [pltpu.VMEM((nz,) + flat, f32)] * 2,
-                [pltpu.VMEM((ng,) + flat, f32)] * 2,
-                [pltpu.VMEM((ng,) + flat, f32)] * 2,
+                [pltpu.VMEM(part, f32) for part in parts],
+                [pltpu.VMEM((nz,) + part, f32) for part in parts],
+                [pltpu.VMEM((ng,) + part, f32) for part in parts],
+                [pltpu.VMEM((ng,) + part, f32) for part in parts],
+                pltpu.VMEM((ROWS, ng * COLS), jnp.bfloat16),
                 pltpu.VMEM(flat, f32),
                 [pltpu.VMEM(flat, f32)] * 2,
                 [pltpu.VMEM(flat, f32)] * 2,
@@ -601,10 +648,10 @@
                 dma((4,)),
                 dma((8,)),
                 dma((8,)),
-                dma((2,)),
-                dma((2,)),
-                dma((2,)),
-                dma((2,)),
+                dma((4,)),
+                dma((4,)),
+                dma((4,)),
+                dma((4,)),
                 dma((2,)),
                 dma((2,)),
             ],
@@ -623,6 +670,14 @@
             partner,
             flip,
         )
+        return pl.pallas_call(
+            hand_out,
+            out_shape=jax.ShapeDtypeStruct(cube, f32),
+            in_specs=[pl.BlockSpec(memory_space=pltpu.VMEM)],
+            out_specs=any_space,
+            scratch_shapes=[dma],
+            compiler_params=pltpu.CompilerParams(vmem_limit_bytes=2**20),
+        )(result)
 
     in_specs = (
         P(None, "tile", "col"),

time: 45.4 us -> 41.8 us (0.921)
  Pallas kernels: 43.5 us -> 41.7 us
  local copies, waits for them, and re-layouts: 1.78 us -> 0 us
    pallas_call x1 -> x2, Pallas kernels: 43.5 us -> 41.7 us  [the longest x1 40.9 us: body(): pl.pallas_call(functools.partial(kernel, n_tile, n_col), out_shape=pltpu....]
    unnamed x1 -> x0, local copies, waits for them, and re-layouts: 1.78 us -> none
where the time goes in v3:
time: 41.8 us; the launch traced here: 41.7 us
  Pallas kernels  41.7 us (100%)
    pallas_call x1, Pallas kernels, body(): pl.pallas_call(functools.partial(kernel, n_tile, n_col), out_shape=pltpu....  40.9 us

profile of v3, /device:TPU:441, one launch (start us, length us, event | category | flops | bytes accessed | tf_op | source)
XLA Modules:
  0.0 41.7 jit_solution(12666404434804545985)
XLA Ops:
  0.0 40.9 %shard_map.100.result = f32[25,32,128]{2,1,0:T(8,128)S(1)} custom-call(f32[25,32,128]{2,1,0:T(8,128)} %adj_h.1, f32[25,32,128]{2,1,0:T(8,128)} %cen_h.1, f32[4,25,32,128]{3,2,1,0:T(8,128)} %side_h.1, f32[2,25,32,128]{3,2,1,0:T(8,128)} %vert_h.1, s32[25,32,128]{2,1,0:T(8,128)} %mask_h.1, f32[4,6,2,1,128]{4,3,2,1,0:T(1,128)} %bitcast.3, ...), custom_call_target="tpu_custom_call" | custom-call | tf_op jit(solution)/shard_map/pallas_call | solution.py:605
  40.9 0.8 %shard_map.101 = f32[25,32,128]{2,1,0:T(8,128)} custom-call(f32[25,32,128]{2,1,0:T(8,128)S(1)} %shard_map.100.result), custom_call_target="tpu_custom_call" | custom-call | tf_op jit(solution)/shard_map/pallas_call | solution.py:673

commit v4 on v3

--- a/solution.py
+++ b/solution.py
@@ -18,6 +18,17 @@
 
 def grid_of(n_col):
     return (4, 6, 2) if n_col == 48 else (2, n_col // 4, 2)
+
+
+def nearest_first(z, nz):
+    short = z * (nz - 1 - z) // 3
+    longer = 1 - 2 * (z // (nz // 2))
+    order = []
+    for k in range(nz):
+        both = (k + 1) // 2 * (1 if k % 2 else -1)
+        two_sided = (2 * short - k + nz) // nz
+        order.append(z + longer * (two_sided * both + (1 - two_sided) * (k - short)))
+    return order
 
 
 def copy_to(src, dst, send, recv, where):
@@ -255,14 +266,14 @@
     loads[3].wait()
     row_ids = lax.broadcasted_iota(jnp.int32, (CELL_ROWS, COLS), 0)
 
-    def columns_of(z, g):
-        return pl.ds(pl.multiple_of((z * ng + g) * COLS, COLS), COLS)
-
-    @pl.loop(0, nz)
-    def _(z):
+    def columns_of(k, g):
+        return pl.ds((k * ng + g) * COLS, COLS)
+
+    order = nearest_first(my_z, nz)
+    for k in range(nz):
         for g in range(ng):
-            hit = row_ids == (cell[g // nc, z, g % nc] >> 7)
-            rows_1h[:, columns_of(z, g)] = jnp.where(hit, f32(1), zero).astype(jnp.bfloat16)
+            hit = row_ids == (cell[g // nc, order[k], g % nc] >> 7)
+            rows_1h[:, columns_of(k, g)] = jnp.where(hit, f32(1), zero).astype(jnp.bfloat16)
 
     loads[0].wait()
     wait_for(plane.at[pl.ds(0, ng - 1)], plane_recv)
@@ -271,18 +282,16 @@
 
         @pl.when(my_z == mine)
         def _():
-            @pl.loop(1, nz)
-            def _(i):
-                z = (mine + i) % nz
+            for z in sorted(range(nz), key=lambda z: -abs(z - mine))[:-1]:
+                k = nearest_first(z, nz).index(mine)
                 copy_to(
                     plane.at[:, z],
-                    slots[mine],
+                    slots[k],
                     slot_send.at[z],
-                    slot_recv.at[mine],
+                    slot_recv.at[k],
                     {"col": on_line(z)},
                 ).start()
-
-            slots[mine][...] = plane[:, mine]
+            slots[0][...] = plane[:, mine]
 
     lane_ids = lax.broadcasted_iota(jnp.int32, (COLS, COLS), 0)
     slot_ids = lax.broadcasted_iota(jnp.int32, (1, COLS), 1)
@@ -333,14 +342,14 @@
     for load in loads[4:]:
         load.wait()
 
-    def add_slots(z, first, last):
-        @pl.when(my_z != z)
-        def _():
-            wait_for(slots[z], slot_recv.at[z])
+    for k in range(nz):
+        z, last = order[k], k == nz - 1
+        if k:
+            wait_for(slots[k], slot_recv.at[k])
 
         for g in range(ng):
             count = cnt_s[(g // nc) * nc * nz + z * nc + g % nc]
-            value = jnp.where(slot_ids < count, slots[z][g], zero)
+            value = jnp.where(slot_ids < count, slots[k][g], zero)
             high = value.astype(jnp.bfloat16).astype(f32)
             hit = lane_ids == (cell[g // nc, z, g % nc] & 127)
             for half, part in enumerate((high, value - high)):
@@ -372,25 +381,15 @@
             pl.when(at_top)(lead)
         width = ng * COLS
         term = lax.dot_general(
-            rows_1h[:, z * width : (z + 1) * width],
+            rows_1h[:, k * width : (k + 1) * width],
             vals_1h[...],
             (((1,), (1,)), ((), ())),
             preferred_element_type=f32,
         )
-        if first:
+        if k:
+            acc[...] += term
+        else:
             acc[...] = term
-        else:
-            acc[...] += term
-
-    @pl.when(my_z < nz // 2)
-    def _():
-        for z in range(nz):
-            add_slots(z, z == 0, z == nz - 1)
-
-    @pl.when(my_z >= nz // 2)
-    def _():
-        for z in range(nz - 1, -1, -1):
-            add_slots(z, z == nz - 1, z == 0)
 
     y_ref[...] = adj[...] + (acc[:, :COLS] + acc[:, COLS:]).reshape(LEVELS, ROWS, COLS)
 

time: 41.8 us -> 39.8 us (0.952)
  Pallas kernels: 41.7 us -> 39.6 us
    pallas_call x1, Pallas kernels: 40.9 us -> 38.9 us  [body(): pl.pallas_call(functools.partial(kernel, n_tile, n_col), out_shape=pltpu....]
where the time goes in v4:
time: 39.8 us; the launch traced here: 39.6 us
  Pallas kernels  39.6 us (99%)
    pallas_call x1, Pallas kernels, body(): pl.pallas_call(functools.partial(kernel, n_tile, n_col), out_shape=pltpu....  38.9 us

profile of v4, /device:TPU:441, one launch (start us, length us, event | category | flops | bytes accessed | tf_op | source)
XLA Modules:
  0.0 39.6 jit_solution(11956292112329303782)
XLA Ops:
  0.0 38.9 %shard_map.100.result = f32[25,32,128]{2,1,0:T(8,128)S(1)} custom-call(f32[25,32,128]{2,1,0:T(8,128)} %adj_h.1, f32[25,32,128]{2,1,0:T(8,128)} %cen_h.1, f32[4,25,32,128]{3,2,1,0:T(8,128)} %side_h.1, f32[2,25,32,128]{3,2,1,0:T(8,128)} %vert_h.1, s32[25,32,128]{2,1,0:T(8,128)} %mask_h.1, f32[4,6,2,1,128]{4,3,2,1,0:T(1,128)} %bitcast.3, ...), custom_call_target="tpu_custom_call" | custom-call | tf_op jit(solution)/shard_map/pallas_call | solution.py:604
  38.9 0.8 %shard_map.101 = f32[25,32,128]{2,1,0:T(8,128)} custom-call(f32[25,32,128]{2,1,0:T(8,128)S(1)} %shard_map.100.result), custom_call_target="tpu_custom_call" | custom-call | tf_op jit(solution)/shard_map/pallas_call | solution.py:672

commit v5 on v4

--- a/solution.py
+++ b/solution.py
@@ -210,7 +210,13 @@
 
     sources = lax.fori_loop(0, n_col, find, (jnp.int32(0),) * (ng + 1))
     my_source = sources[ng]
-    flipped = ff_s[my_source]
+
+    def find_again(s, found):
+        target = fp_s[s]
+        return tuple(jnp.where(target == sources[g], s, found[g]) for g in range(ng + 1))
+
+    sources_2 = lax.fori_loop(0, n_col, find_again, (jnp.int32(0),) * (ng + 1))
+    my_source_2 = sources_2[ng]
 
     lanes = lax.broadcasted_iota(jnp.int32, (LEVELS, ROWS, COLS), 2)
     rows = lax.broadcasted_iota(jnp.int32, (LEVELS, ROWS, COLS), 1)
@@ -232,6 +238,54 @@
         spread = jnp.where(q_lane == q_id, tile[None], zero)
         return jnp.sum(spread, axis=2, keepdims=True).reshape(LEVELS, ROWS, 1)
 
+    def fold_start(n, h):
+        part = 2 * n + h
+        line_bufs[part][my_z] = fold_out[part][...]
+
+        @pl.loop(1, nz)
+        def _(i):
+            z = (my_z + nz + far_way * (nz - i)) % nz
+            copy_to(
+                fold_out[part],
+                line_bufs[part].at[my_z],
+                line_send.at[part],
+                line_recv.at[part],
+                {"col": on_line(z)},
+            ).start()
+
+    def fold_wait(n, h):
+        part = 2 * n + h
+        wait_for(line_bufs[part].at[pl.ds(0, nz - 1)], line_recv.at[part])
+
+    def fold_pick(n, h, chosen, to):
+        part, end = 2 * n + h, 2 * to + h
+        for g in range(ng):
+            pick_bufs[end][g] = line_bufs[part][(chosen[g] // nc) % nz]
+
+        @pl.loop(1, ng)
+        def _(i):
+            g = (my_g + i) % ng
+            copy_to(
+                pick_bufs[end].at[g],
+                group_bufs[end].at[my_g],
+                pick_send.at[end],
+                pick_recv.at[end],
+                {"col": in_plane(g)},
+            ).start()
+
+        group_bufs[end][my_g] = pick_bufs[end][my_g]
+
+    def fold_finish(n, h, source, turns):
+        end = 2 * n + h
+        count = PARTS[h][1] - PARTS[h][0]
+        wait_for(group_bufs[end].at[pl.ds(0, ng - 1)], pick_recv.at[end])
+        arrived = group_bufs[end][(source // (nc * nz)) * nc + source % nc]
+        backwards = COLS - 1 - lax.broadcasted_iota(jnp.int32, (count, COLS), 1)
+        for column in turns:
+            turned = jnp.take_along_axis(arrived, backwards, axis=1)
+            arrived = jnp.where(ff_s[column] == 1, turned, arrived)
+        return arrived
+
     loads[1].wait()
     loads[2].wait()
     ocean = mask[...].astype(f32)
@@ -259,6 +313,12 @@
         )
         for way in range(2)
     ]
+    @pl.when(at_top)
+    def _():
+        for h, (low, high) in enumerate(PARTS):
+            fold_out[4 + h][...] = fixed_row[0][low:high, :]
+            fold_start(2, h)
+
     for way in range(2):
         fixed[way].start()
         pl.when(can_go[way])(fixed[2 + way].start)
@@ -295,49 +355,6 @@
 
     lane_ids = lax.broadcasted_iota(jnp.int32, (COLS, COLS), 0)
     slot_ids = lax.broadcasted_iota(jnp.int32, (1, COLS), 1)
-
-    def fold_start(n, h):
-        part = 2 * n + h
-        line_bufs[part][my_z] = fold_out[part][...]
-
-        @pl.loop(1, nz)
-        def _(i):
-            z = (my_z + nz + far_way * (nz - i)) % nz
-            copy_to(
-                fold_out[part],
-                line_bufs[part].at[my_z],
-                line_send.at[part],
-                line_recv.at[part],
-                {"col": on_line(z)},
-            ).start()
-
-    def fold_pick(n, h):
-        part = 2 * n + h
-        wait_for(line_bufs[part].at[pl.ds(0, nz - 1)], line_recv.at[part])
-        for g in range(ng):
-            pick_bufs[part][g] = line_bufs[part][(sources[g] // nc) % nz]
-
-        @pl.loop(1, ng)
-        def _(i):
-            g = (my_g + i) % ng
-            copy_to(
-                pick_bufs[part].at[g],
-                group_bufs[part].at[my_g],
-                pick_send.at[part],
-                pick_recv.at[part],
-                {"col": in_plane(g)},
-            ).start()
-
-        group_bufs[part][my_g] = pick_bufs[part][my_g]
-
-    def fold_finish(n, h):
-        part = 2 * n + h
-        count = PARTS[h][1] - PARTS[h][0]
-        wait_for(group_bufs[part].at[pl.ds(0, ng - 1)], pick_recv.at[part])
-        arrived = group_bufs[part][(my_source // (nc * nz)) * nc + my_source % nc]
-        backwards = COLS - 1 - lax.broadcasted_iota(jnp.int32, (count, COLS), 1)
-        turned = jnp.take_along_axis(arrived, backwards, axis=1)
-        return jnp.where(flipped == 1, turned, arrived)
 
     for load in loads[4:]:
         load.wait()
@@ -473,7 +490,13 @@
     @pl.when(at_top)
     def _():
         for h in range(2):
-            fold_pick(0, h)
+            fold_wait(2, h)
+            fold_pick(2, h, sources, 2)
+        for h in range(2):
+            fold_wait(0, h)
+            fold_pick(0, h, sources, 0)
+        for h in range(2):
+            fold_pick(0, h, sources_2, 3)
 
     for way in range(2):
         halos[way].wait_recv()
@@ -510,10 +533,12 @@
     @pl.when(at_top)
     def _():
         for h, (low, high) in enumerate(PARTS):
-            edge = mask[low:high, top, :].astype(f32) * fold_finish(0, h)
-            delta[low:high, :] = edge
-            fold_out[2 + h][...] = side[2, low:high, top, :] * (y_ref[low:high, top, :] + edge)
+            fold_out[2 + h][...] = side[2, low:high, top, :] * y_ref[low:high, top, :]
             fold_start(1, h)
+        for h, (low, high) in enumerate(PARTS):
+            delta[low:high, :] = mask[low:high, top, :].astype(f32) * fold_finish(
+                0, h, my_source, [my_source]
+            )
         for way in range(2):
             delta_out[way][...] = side[way, :, top, :] * delta[...]
             moves[way].start()
@@ -558,17 +583,23 @@
         below = side[3, :, top, :] * delta[...]
         out_ref[:, top - 1, :] = out_ref[:, top - 1, :] + below * mask[:, top - 1, :].astype(f32)
         delta[...] = change
+        for h, (low, high) in enumerate(PARTS):
+            delta[low:high, :] = delta[low:high, :] + fold_finish(
+                2, h, my_source, [my_source]
+            ) * fold_finish(3, h, my_source_2, [my_source_2, my_source])
         for h in range(2):
-            fold_pick(1, h)
+            fold_wait(1, h)
+            fold_pick(1, h, sources, 1)
         for h, (low, high) in enumerate(PARTS):
-            total = delta[low:high, :] + fold_finish(1, h)
+            total = delta[low:high, :] + fold_finish(1, h, my_source, [my_source])
             out_ref[low:high, top, :] = out_ref[low:high, top, :] + total * mask[
                 low:high, top, :
             ].astype(f32)
         for way in range(2):
             moves[way].wait_send()
-        for part in range(4):
+        for part in range(6):
             wait_for(line_bufs[part].at[pl.ds(0, nz - 1)], line_send.at[part])
+        for part in range(8):
             wait_for(group_bufs[part].at[pl.ds(0, ng - 1)], pick_send.at[part])
 
     wait_for(plane.at[pl.ds(0, ng - 1)], plane_send)
@@ -594,7 +625,7 @@
     ng = nx * nc
     cube = (LEVELS, ROWS, COLS)
     flat = (LEVELS, COLS)
-    parts = [(high - low, COLS) for low, high in PARTS] * 2
+    parts = [(high - low, COLS) for low, high in PARTS]
     f32 = jnp.float32
     any_space = pl.BlockSpec(memory_space=pl.ANY)
     scalars = pl.BlockSpec(memory_space=pltpu.SMEM)
@@ -630,10 +661,10 @@
                 [pltpu.VMEM((2, 8, COLS), f32)] * 2,
                 [pltpu.VMEM((8, COLS), f32)] * 4,
                 [pltpu.VMEM((8, COLS), f32)] * 4,
-                [pltpu.VMEM(part, f32) for part in parts],
-                [pltpu.VMEM((nz,) + part, f32) for part in parts],
-                [pltpu.VMEM((ng,) + part, f32) for part in parts],
-                [pltpu.VMEM((ng,) + part, f32) for part in parts],
+                [pltpu.VMEM(part, f32) for part in parts * 3],
+                [pltpu.VMEM((nz,) + part, f32) for part in parts * 3],
+                [pltpu.VMEM((ng,) + part, f32) for part in parts * 4],
+                [pltpu.VMEM((ng,) + part, f32) for part in parts * 4],
                 pltpu.VMEM((ROWS, ng * COLS), jnp.bfloat16),
                 pltpu.VMEM(flat, f32),
                 [pltpu.VMEM(flat, f32)] * 2,
@@ -647,10 +678,10 @@
                 dma((4,)),
                 dma((8,)),
                 dma((8,)),
-                dma((4,)),
-                dma((4,)),
-                dma((4,)),
-                dma((4,)),
+                dma((6,)),
+                dma((6,)),
+                dma((8,)),
+                dma((8,)),
                 dma((2,)),
                 dma((2,)),
             ],

time: 39.8 us -> 39.8 us (level)
  no operation moved by 1% of the time
where the time goes in v5:
time: 39.8 us; the launch traced here: 39.7 us
  Pallas kernels  39.7 us (100%)
    pallas_call x1, Pallas kernels, body(): pl.pallas_call(functools.partial(kernel, n_tile, n_col), out_shape=pltpu....  38.9 us

profile of v5, /device:TPU:441, one launch (start us, length us, event | category | flops | bytes accessed | tf_op | source)
XLA Modules:
  0.0 39.7 jit_solution(8851815697773688882)
XLA Ops:
  0.0 38.9 %shard_map.100.result = f32[25,32,128]{2,1,0:T(8,128)S(1)} custom-call(f32[25,32,128]{2,1,0:T(8,128)} %adj_h.1, f32[25,32,128]{2,1,0:T(8,128)} %cen_h.1, f32[4,25,32,128]{3,2,1,0:T(8,128)} %side_h.1, f32[2,25,32,128]{3,2,1,0:T(8,128)} %vert_h.1, s32[25,32,128]{2,1,0:T(8,128)} %mask_h.1, f32[4,6,2,1,128]{4,3,2,1,0:T(1,128)} %bitcast.3, ...), custom_call_target="tpu_custom_call" | custom-call | tf_op jit(solution)/shard_map/pallas_call | solution.py:635
  39.0 0.8 %shard_map.101 = f32[25,32,128]{2,1,0:T(8,128)} custom-call(f32[25,32,128]{2,1,0:T(8,128)S(1)} %shard_map.100.result), custom_call_target="tpu_custom_call" | custom-call | tf_op jit(solution)/shard_map/pallas_call | solution.py:703

commit v6 on v5

--- a/solution.py
+++ b/solution.py
@@ -361,6 +361,14 @@
 
     for k in range(nz):
         z, last = order[k], k == nz - 1
+        if last:
+
+            @pl.when(at_top)
+            def _():
+                for h in range(2):
+                    fold_wait(2, h)
+                    fold_pick(2, h, sources, 2)
+
         if k:
             wait_for(slots[k], slot_recv.at[k])
 
@@ -487,17 +495,6 @@
             for copy in far[way]:
                 copy.start()
 
-    @pl.when(at_top)
-    def _():
-        for h in range(2):
-            fold_wait(2, h)
-            fold_pick(2, h, sources, 2)
-        for h in range(2):
-            fold_wait(0, h)
-            fold_pick(0, h, sources, 0)
-        for h in range(2):
-            fold_pick(0, h, sources_2, 3)
-
     for way in range(2):
         halos[way].wait_recv()
         fixed[way].wait_recv()
@@ -535,6 +532,11 @@
         for h, (low, high) in enumerate(PARTS):
             fold_out[2 + h][...] = side[2, low:high, top, :] * y_ref[low:high, top, :]
             fold_start(1, h)
+        for h in range(2):
+            fold_wait(0, h)
+            fold_pick(0, h, sources, 0)
+        for h in range(2):
+            fold_pick(0, h, sources_2, 3)
         for h, (low, high) in enumerate(PARTS):
             delta[low:high, :] = mask[low:high, top, :].astype(f32) * fold_finish(
                 0, h, my_source, [my_source]

time: 39.8 us -> 42.2 us (1.060)
  Pallas kernels: 39.7 us -> 42 us
    pallas_call x1, Pallas kernels: 38.9 us -> 41.2 us  [body(): pl.pallas_call(functools.partial(kernel, n_tile, n_col), out_shape=pltpu....]
where the time goes in v6:
time: 42.2 us; the launch traced here: 42 us
  Pallas kernels  42 us (100%)
    pallas_call x1, Pallas kernels, body(): pl.pallas_call(functools.partial(kernel, n_tile, n_col), out_shape=pltpu....  41.2 us

profile of v6, /device:TPU:441, one launch (start us, length us, event | category | flops | bytes accessed | tf_op | source)
XLA Modules:
  0.0 42.0 jit_solution(2012092059208897837)
XLA Ops:
  0.0 41.2 %shard_map.100.result = f32[25,32,128]{2,1,0:T(8,128)S(1)} custom-call(f32[25,32,128]{2,1,0:T(8,128)} %adj_h.1, f32[25,32,128]{2,1,0:T(8,128)} %cen_h.1, f32[4,25,32,128]{3,2,1,0:T(8,128)} %side_h.1, f32[2,25,32,128]{3,2,1,0:T(8,128)} %vert_h.1, s32[25,32,128]{2,1,0:T(8,128)} %mask_h.1, f32[4,6,2,1,128]{4,3,2,1,0:T(1,128)} %bitcast.3, ...), custom_call_target="tpu_custom_call" | custom-call | tf_op jit(solution)/shard_map/pallas_call | solution.py:637
  41.3 0.8 %shard_map.101 = f32[25,32,128]{2,1,0:T(8,128)} custom-call(f32[25,32,128]{2,1,0:T(8,128)S(1)} %shard_map.100.result), custom_call_target="tpu_custom_call" | custom-call | tf_op jit(solution)/shard_map/pallas_call | solution.py:705

commit v7 on v6

--- a/solution.py
+++ b/solution.py
@@ -495,6 +495,12 @@
             for copy in far[way]:
                 copy.start()
 
+    @pl.when(at_top)
+    def _():
+        for h in range(2):
+            fold_wait(0, h)
+            fold_pick(0, h, sources, 0)
+
     for way in range(2):
         halos[way].wait_recv()
         fixed[way].wait_recv()
@@ -532,9 +538,6 @@
         for h, (low, high) in enumerate(PARTS):
             fold_out[2 + h][...] = side[2, low:high, top, :] * y_ref[low:high, top, :]
             fold_start(1, h)
-        for h in range(2):
-            fold_wait(0, h)
-            fold_pick(0, h, sources, 0)
         for h in range(2):
             fold_pick(0, h, sources_2, 3)
         for h, (low, high) in enumerate(PARTS):

time: 42.2 us -> 40.5 us (0.960)
  Pallas kernels: 42 us -> 40.4 us
    pallas_call x1, Pallas kernels: 41.2 us -> 39.6 us  [body(): pl.pallas_call(functools.partial(kernel, n_tile, n_col), out_shape=pltpu....]
where the time goes in v7:
time: 40.5 us; the launch traced here: 40.4 us
  Pallas kernels  40.4 us (100%)
    pallas_call x1, Pallas kernels, body(): pl.pallas_call(functools.partial(kernel, n_tile, n_col), out_shape=pltpu....  39.6 us

profile of v7, /device:TPU:441, one launch (start us, length us, event | category | flops | bytes accessed | tf_op | source)
XLA Modules:
  0.0 40.4 jit_solution(2043841933320737960)
XLA Ops:
  0.0 39.6 %shard_map.100.result = f32[25,32,128]{2,1,0:T(8,128)S(1)} custom-call(f32[25,32,128]{2,1,0:T(8,128)} %adj_h.1, f32[25,32,128]{2,1,0:T(8,128)} %cen_h.1, f32[4,25,32,128]{3,2,1,0:T(8,128)} %side_h.1, f32[2,25,32,128]{3,2,1,0:T(8,128)} %vert_h.1, s32[25,32,128]{2,1,0:T(8,128)} %mask_h.1, f32[4,6,2,1,128]{4,3,2,1,0:T(1,128)} %bitcast.3, ...), custom_call_target="tpu_custom_call" | custom-call | tf_op jit(solution)/shard_map/pallas_call | solution.py:640
  39.6 0.8 %shard_map.101 = f32[25,32,128]{2,1,0:T(8,128)} custom-call(f32[25,32,128]{2,1,0:T(8,128)S(1)} %shard_map.100.result), custom_call_target="tpu_custom_call" | custom-call | tf_op jit(solution)/shard_map/pallas_call | solution.py:708
